TPU v7x, 32 devices: a whole 2x2x4 slice. The times are simulated.
32 devices in a mesh: shot: 4 (over y, core), space: 8 (over z, x).
Axes of the slice: x: 2, y: 2, z: 4, core: 2. Of those that a mesh axis runs over, the one named last changes fastest.
Arguments:
- adjoint_now: float32 [4, 128, 64, 512], P('shot', 'space'), may hold values from -6 to 6
- adjoint_later: float32 [4, 128, 64, 512], P('shot', 'space'), may hold values from -6 to 6
- courant: float32 [128, 64, 512], P('space'), may hold values from 0.05 to 0.2
- checkpoint_codes: int32 [4, 6, 128, 64, 128], P('shot', None, 'space'), may hold values from -2147483648 to 2147483646
- scale_index: int32 [4, 6, 128, 256], P('shot', None, 'space'), may hold values from 0 to 63
- scale_table: float32 [64], replicated, may hold values from 0.001 to 0.01
- receiver_cell: int32 [4, 2048], P('shot', 'space'), may hold values from 0 to 4194303, as said below
- observed: float32 [4, 4, 2048], P('shot', None, 'space'), may hold values from -12 to 12
- source_cell: int32 [4, 3], P('shot'), may hold values from 0 to 511, as said below
Outputs:
- gradient: float32 [128, 64, 512], P('space', 'shot')
- adjoint_first: float32 [4, 128, 64, 512], P('shot', 'space')
- adjoint_second: float32 [4, 128, 64, 512], P('shot', 'space')
- misfit: float32 [], replicated
Inputs may be any that keep to these rules, and one draw needn't show every extreme that they name: `receiver_cell`: for every r, entries r * 256 to (r + 1) * 256 - 1 of each shot's row are flat indices (z * 64 + y) * 512 + x of cells with r * 16 <= z < (r + 1) * 16. `source_cell`: column 0 is a z index below 128, column 1 a y index below 64, column 2 an x index below 512.
All inputs are finite; a program needn't handle non-finite values.
Results may differ from a plain program's by a relative error of at most 0.0001.
Values sent between devices are 32-bit elements; how exact they have to be, the bound alone decides.
No kernel may reach another device: no remote copies, remote signals or barrier semaphores. Data moves between devices by JAX's collectives and lax.ppermute only.
A program may use at most 128 MiB of HBM per device.

v0:
```python
import jax
import jax.numpy as jnp
from jax import lax
from jax.sharding import PartitionSpec as P

ITERS = 4
QBLOCK = 128
MUTE = 8


COEFFS = (-205.0 / 72.0, 8.0 / 5.0, -1.0 / 5.0, 8.0 / 315.0, -1.0 / 560.0)


def with_halo(block, sides, width):
    for axis, dim in sides:
        count = lax.axis_size(axis)
        forward = [(i, i + 1) for i in range(count - 1)]
        backward = [(target, source) for source, target in forward]
        low = lax.ppermute(
            lax.slice_in_dim(block, block.shape[dim] - width, None, axis=dim), axis, forward
        )
        high = lax.ppermute(lax.slice_in_dim(block, 0, width, axis=dim), axis, backward)
        block = jnp.concatenate([low, block, high], axis=dim)
    return block


def decode(words, index, table):
    planes = [jnp.bitwise_and(jnp.right_shift(words, 8 * m), 255) for m in range(4)]
    codes = jnp.concatenate(planes, axis=-1)
    centred = (codes - 128).astype(jnp.float32)
    depth, rows, cols = centred.shape
    onehot = index[..., None] == jnp.arange(table.shape[0], dtype=jnp.int32)
    scale = jnp.sum(jnp.where(onehot, table, 0.0), axis=-1)
    blocks = centred.reshape(depth, rows, cols // QBLOCK, QBLOCK) * scale.reshape(
        depth, rows, cols // QBLOCK, 1
    )
    return blocks.reshape(depth, rows, cols)


def laplace(field):
    depth, rows, cols = field.shape
    deep = with_halo(field, (("space", 0),), 4)
    flat = jnp.pad(field, ((0, 0), (4, 4), (4, 4)))
    total = 3.0 * COEFFS[0] * field
    for step in range(1, 5):
        total = total + COEFFS[step] * (
            deep[4 + step : 4 + step + depth] + deep[4 - step : 4 - step + depth]
        )
        total = total + COEFFS[step] * (
            flat[:, 4 + step : 4 + step + rows, 4 : 4 + cols]
            + flat[:, 4 - step : 4 - step + rows, 4 : 4 + cols]
        )
        total = total + COEFFS[step] * (
            flat[:, 4 : 4 + rows, 4 + step : 4 + step + cols]
            + flat[:, 4 : 4 + rows, 4 - step : 4 - step + cols]
        )
    return total


def body(
    adjoint_now,
    adjoint_later,
    courant,
    checkpoint_codes,
    scale_index,
    scale_table,
    receiver_cell,
    observed,
    source_cell,
):
    now = adjoint_now[0]
    later = adjoint_later[0]
    depth, rows, cols = now.shape
    first_z = lax.axis_index("space") * depth
    cells = receiver_cell[0] - first_z * (rows * cols)
    fields = [
        decode(checkpoint_codes[0, level], scale_index[0, level], scale_table)
        for level in range(ITERS + 2)
    ]
    image = jnp.zeros((depth, rows, cols), jnp.float32)
    misfit_part = jnp.zeros((), jnp.float32)
    for step in range(ITERS):
        level = ITERS - step
        synthetic = jnp.take(fields[level].reshape(-1), cells)
        residual = synthetic - observed[0, level - 1]
        misfit_part = misfit_part + jnp.sum(residual * residual)
        image = image + now * (fields[level + 1] - 2.0 * fields[level] + fields[level - 1])
        stepped = 2.0 * now - later + courant * laplace(now)
        stepped = stepped.reshape(-1).at[cells].add(residual).reshape(depth, rows, cols)
        later = now
        now = stepped
    source = source_cell[0]
    zpos = (first_z + jnp.arange(depth, dtype=jnp.int32)).reshape(depth, 1, 1)
    ypos = jnp.arange(rows, dtype=jnp.int32).reshape(1, rows, 1)
    xpos = jnp.arange(cols, dtype=jnp.int32).reshape(1, 1, cols)
    dist = ((zpos - source[0]) ** 2 + (ypos - source[1]) ** 2 + (xpos - source[2]) ** 2).astype(
        jnp.float32
    )
    muted = image * (1.0 - jnp.exp(-dist / (2.0 * MUTE * MUTE)))
    gradient = lax.psum_scatter(muted, "shot", scatter_dimension=1, tiled=True)
    count = lax.axis_size("shot") * ITERS * receiver_cell.shape[1] * lax.axis_size("space")
    misfit = 0.5 * lax.psum(misfit_part, ("shot", "space")) / count
    return (gradient, now[None], later[None], misfit)


def solution(mesh):
    placed = (
        P("shot", "space", None, None),
        P("shot", "space", None, None),
        P("space", None, None),
        P("shot", None, "space", None, None),
        P("shot", None, "space", None),
        P(),
        P("shot", "space"),
        P("shot", None, "space"),
        P("shot", None),
    )
    return jax.shard_map(
        body,
        mesh=mesh,
        in_specs=placed,
        out_specs=(
            P("space", "shot", None),
            P("shot", "space", None, None),
            P("shot", "space", None, None),
            P(),
        ),
        check_vma=False,
    )
```

profile of v0, /device:TPU:0, one launch (start us, length us, event | category | flops | bytes accessed | tf_op | source)
XLA Modules:
  0.0 308.5 jit_solution(9114764034815318383)
XLA Ops:
  10.8 6.3 %collective-permute-start.1 = (f32[4,64,512]{2,1,0:T(8,128)}, f32[4,64,512]{2,1,0:T(8,128)}, u32[]{:S(2)}, u32[]{:S(2)}) collective-permute-start(f32[4,64,512]{2,1,0:T(8,128)} %get-tuple-element.59), channel_id=1, source_target_pairs={{0,1},{1,2},{2,3},{3,4},{4,5},{5,6},{6,7},{8,9},{9,10},{10,11},{11... | collective-permute-start | bytes 1572872 | tf_op jit(solution)/shard_map/ppermute | solution.py:19
  17.1 3.3 %and_bitcast_fusion.7 = (s32[16,64,1,128]{3,1,0,2:T(8,128)}, s32[16,64,1,128]{3,1,0,2:T(8,128)}, s32[16,64,1,128]{3,1,0,2:T(8,128)}, s32[16,64,1,128]{3,1,0,2:T(8,128)}, s32[16,64,1,128]{3,1,0,2:T(8,128)S(1)}) fusion(s32[1,6,16,64,128]{4,3,2,1,0:T(8,128)} %param.14), kind=kLoop, calls=%fused_computation.304 | loop fusion | flops 1310720 | bytes 5242880 | tf_op jit(solution)/shard_map/and | solution.py:28
  20.4 3.7 %and_bitcast_fusion.23 = (s32[16,64,1,128]{3,1,0,2:T(8,128)S(1)}, s32[16,64,1,128]{3,1,0,2:T(8,128)}, s32[16,64,1,128]{3,1,0,2:T(8,128)}, s32[16,64,1,128]{3,1,0...) fusion(s32[1,6,16,64,128]{4,3,2,1,0:T(8,128)S(1)} %copy-done.11), kind=kLoop, calls=%fused_computation.322 | loop fusion | flops 4980736 | bytes 13107200 | tf_op jit(solution)/shard_map/and | solution.py:28
  26.5 3.9 %fusion.162 = (f32[16,64,4,128]{3,1,0,2:T(8,128)S(1)}, f32[16,64,4,128]{3,1,0,2:T(8,128)S(1)}) fusion(s32[16,64,1,128]{3,1,0,2:T(8,128)} %get-tuple-element.27, s32[16,64,1,128]{3,1,0,2:T(8,128)} %get-tuple-element.26, s32[16,64,1,128]{3,1,0,2:T(8,128)} %get-tuple-element.25, s32[16,64,1,128]{3,1,0,2:T(8,128)} %get-tuple-element.43, ...), kind=kLoop, calls=%fused_computation.270 | loop fusion | flops 6291456 | bytes 8421376 | tf_op jit(solution)/shard_map/mul | solution.py:34
  30.3 2.8 copy.40
  33.2 2.7 copy.43
  36.0 2.6 fusion.166
  38.6 3.4 %gather_fusion = f32[256]{0:T(256)S(1)} fusion(f32[524288]{0:T(1024)} %bitcast.181, s32[1024]{0:T(1024)S(1)} %pad_clamp_fusion), kind=kCustom, calls=%fused_computation.clone | custom fusion | bytes 3072 | tf_op jit(solution)/shard_map/jit(_take)/gather | solution.py:84
  42.0 3.5 %gather_fusion.1 = f32[256]{0:T(256)S(1)} fusion(f32[524288]{0:T(1024)} %bitcast.182, s32[1024]{0:T(1024)S(1)} %pad_clamp_fusion), kind=kCustom, calls=%fused_computation.1.clone | custom fusion | bytes 3072 | tf_op jit(solution)/shard_map/jit(_take)/gather | solution.py:84
  45.5 2.7 copy.47
  48.2 3.5 %gather_fusion.2 = f32[256]{0:T(256)S(1)} fusion(f32[524288]{0:T(1024)} %bitcast.184, s32[1024]{0:T(1024)S(1)} %pad_clamp_fusion), kind=kCustom, calls=%fused_computation.2.clone | custom fusion | bytes 3072 | tf_op jit(solution)/shard_map/jit(_take)/gather | solution.py:84
  51.7 4.5 %copy.51 = f32[16,64,4,128]{3,2,1,0:T(4,128)} copy(f32[16,64,4,128]{3,1,0,2:T(8,128)} %get-tuple-element.84) | data formatting | bytes 4194304 | tf_op jit(solution)/shard_map/mul | solution.py:34
  56.2 3.5 %gather_fusion.3 = f32[256]{0:T(256)S(1)} fusion(f32[524288]{0:T(1024)} %bitcast.183, s32[1024]{0:T(1024)S(1)} %pad_clamp_fusion), kind=kCustom, calls=%fused_computation.3.clone | custom fusion | bytes 3072 | tf_op jit(solution)/shard_map/jit(_take)/gather | solution.py:84
  60.3 29.2 %fusion.10 = f32[16,64,512]{2,1,0:T(8,128)S(1)} fusion(f32[16,64,512]{2,1,0:T(8,128)S(1)} %copy-done.2, f32[16,64,512]{2,1,0:T(8,128)} %bitcast.173, f32[4,64,512]{2,1,0:T(8,128)} %collective-permute-done.1, f32[4,64,512]{2,1,0:T(8,128)} %collective-permute-done, f32[1,16,64,512]{3,2,1,0:T(8,128)} %param.12), kind=kLoop, calls=%fused_computation.94 | loop fusion | flops 25690112 | bytes 9437184 | tf_op jit(solution)/shard_map/add | solution.py:88
  90.1 2.9 scatter_fusion
  96.1 4.8 %collective-permute-start.3 = (f32[4,64,512]{2,1,0:T(8,128)}, f32[4,64,512]{2,1,0:T(8,128)}, u32[]{:S(2)}, u32[]{:S(2)}) collective-permute-start(f32[4,64,512]{2,1,0:T(8,128)} %slice.517), channel_id=1, source_target_pairs={{0,1},{1,2},{2,3},{3,4},{4,5},{5,6},{6,7},{8,9},{9,10},{10,11},{11... | collective-permute-start | bytes 1572872 | tf_op jit(solution)/shard_map/ppermute | solution.py:19
  105.9 16.4 %collective-permute-done.3 = f32[4,64,512]{2,1,0:T(8,128)} collective-permute-done((f32[4,64,512]{2,1,0:T(8,128)}, f32[4,64,512]{2,1,0:T(8,128)}, u32[]{:S(2)}, u32[]{:S(2)}) %collective-permute-start.3) | collective-permute-done | bytes 524320 | tf_op jit(solution)/shard_map/ppermute | solution.py:19
  125.8 4.9 %fusion.56 = f32[16,64,512]{2,1,0:T(8,128)S(1)} fusion(f32[16,64,512]{2,1,0:T(8,128)S(1)} %copy-done.3, f32[16,64,512]{2,1,0:T(8,128)S(1)} %reshape.603, f32[20,64,512]{2,1,0:T(8,128)S(1)} %get-tuple-element.57, f32[20,64,512]{2,1,0:T(8,128)S(1)} %constant_dynamic-update-slice_fusion, f32[1,16,64,512]{3,2,1,0:T(8,128)S(1)} %copy-done.6), kind=kLoop, calls=%fused_computation.140 | loop fusion | flops 21495808 | bytes 25165824 | tf_op jit(solution)/shard_map/add | solution.py:88
  132.5 4.8 %scatter_fusion.1 = f32[524288]{0:T(1024)} fusion(f32[524288]{0:T(1024)} %bitcast.175, s32[256]{0:T(256)S(1)} %bitcast.192, f32[256]{0:T(256)S(1)} %get-tuple-element.71), kind=kCustom, calls=%fused_computation.5 | custom fusion | flops 256 | bytes 4096 | tf_op jit(solution)/shard_map/scatter-add | solution.py:89
  141.5 5.2 %collective-permute-start.5 = (f32[4,64,512]{2,1,0:T(8,128)}, f32[4,64,512]{2,1,0:T(8,128)}, u32[]{:S(2)}, u32[]{:S(2)}) collective-permute-start(f32[4,64,512]{2,1,0:T(8,128)} %slice.548), channel_id=1, source_target_pairs={{0,1},{1,2},{2,3},{3,4},{4,5},{5,6},{6,7},{8,9},{9,10},{10,11},{11... | collective-permute-start | bytes 1572872 | tf_op jit(solution)/shard_map/ppermute | solution.py:19
  152.8 2.8 reshape.605
  155.6 11.6 %collective-permute-done.5 = f32[4,64,512]{2,1,0:T(8,128)} collective-permute-done((f32[4,64,512]{2,1,0:T(8,128)}, f32[4,64,512]{2,1,0:T(8,128)}, u32[]{:S(2)}, u32[]{:S(2)}) %collective-permute-start.5) | collective-permute-done | bytes 524320 | tf_op jit(solution)/shard_map/ppermute | solution.py:19
  171.6 5.0 %fusion.85 = f32[16,64,512]{2,1,0:T(8,128)S(1)} fusion(f32[16,64,512]{2,1,0:T(8,128)S(1)} %copy-done.4, f32[16,64,512]{2,1,0:T(8,128)S(1)} %copy-done, f32[20,64,512]{2,1,0:T(8,128)S(1)} %get-tuple-element.53, f32[20,64,512]{2,1,0:T(8,128)S(1)} %constant_dynamic-update-slice_fusion.4, f32[16,64,512]{2,1,0:T(8,128)S(1)} %reshape.603), kind=kLoop, calls=%fused_computation.169 | loop fusion | flops 21495808 | bytes 25165824 | tf_op jit(solution)/shard_map/add | solution.py:88
  178.5 4.8 %scatter_fusion.2 = f32[524288]{0:T(1024)} fusion(f32[524288]{0:T(1024)} %bitcast.172, s32[256]{0:T(256)S(1)} %bitcast.193, f32[256]{0:T(256)S(1)} %get-tuple-element.73), kind=kCustom, calls=%fused_computation.6 | custom fusion | flops 256 | bytes 4096 | tf_op jit(solution)/shard_map/scatter-add | solution.py:89
  187.4 5.2 %collective-permute-start.7 = (f32[4,64,512]{2,1,0:T(8,128)}, f32[4,64,512]{2,1,0:T(8,128)}, u32[]{:S(2)}, u32[]{:S(2)}) collective-permute-start(f32[4,64,512]{2,1,0:T(8,128)} %slice.582), channel_id=1, source_target_pairs={{0,1},{1,2},{2,3},{3,4},{4,5},{5,6},{6,7},{8,9},{9,10},{10,11},{11... | collective-permute-start | bytes 1572872 | tf_op jit(solution)/shard_map/ppermute | solution.py:19
  192.7 5.2 %fusion.160 = (f32[4,16,8,8,128]{4,3,2,1,0:T(8,128)}, f32[4,16,8,8,128]{4,3,2,1,0:T(8,128)}) fusion(s32[16,64,1,128]{3,1,0,2:T(8,128)} %get-tuple-element.24, s32[16,64,1,128]{3,1,0,2:T(8,128)} %get-tuple-element.23, s32[16,64,1,128]{3,1,0,2:T(8,128)} %get-tuple-element.22, s32[16,64,1,128]{3,1,0,2:T(8,128)S(1)} %get-tuple-element.21, ...), kind=kLoop, calls=%fused_computation.267 | loop fusion | flops 6291456 | bytes 8421376
  197.9 2.8 reshape.607
  202.1 9.6 %constant_dynamic-update-slice_fusion.9 = (f32[20,64,512]{2,1,0:T(8,128)}, f32[20,64,512]{2,1,0:T(8,128)S(1)}, f32[16,64,512]{2,1,0:T(8,128)}) fusion(f32[16,64,512]{2,1,0:T(8,128)} %reshape.607, f32[20,64,512]{2,1,0:T(8,128)S(1)} %constant_dynamic-update-slice_fusion.11, s32[512]{0:T(512)S(1)} %subtract_multiply_fusion, ...), kind=kLoop, calls=%fused_computation.332 | loop fusion | flops 13107199 | bytes 27273216
  218.3 46.7 %psum.7 = f32[]{:T(128)} all-reduce(f32[]{:T(128)S(6)} %add.560), channel_id=1, replica_groups=mesh['shot'=4,'space'=8] {'shot','space'}, use_global_device_ids=true, to_apply=%region_15.17 | all-reduce | flops 1 | bytes 8 | tf_op jit(solution)/shard_map/psum | solution.py:102
  265.7 2.9 broadcast_in_dim_reshape.7
  269.4 26.3 %fusion.114 = f32[16,64,512]{2,1,0:T(8,128)S(1)} fusion(f32[16,64,512]{2,1,0:T(8,128)} %param.13, f32[16,64,512]{2,1,0:T(8,128)} %reshape.607, f32[20,64,512]{2,1,0:T(8,128)} %copy-done.5, f32[20,64,512]{2,1,0:T(8,128)} %constant_dynamic-update-slice_fusion.8, f32[16,64,512]{2,1,0:T(8,128)S(1)} %copy-done.1), kind=kLoop, calls=%fused_computation.198 | loop fusion | flops 21495808 | bytes 25165824 | tf_op jit(solution)/shard_map/add | solution.py:88
  296.3 2.7 scatter_fusion.3
  (113 shorter events, 49.7 us)
Async XLA Ops:
  7.2 293.3 %reduce-scatter.2.cloned.1.call-start = ((), (), s32[]{:S(2)}) async-start(), calls=%async_computation.1 | async-start | bytes 2621440 | tf_op jit(solution)/shard_map/reduce_scatter | solution.py:100
  9.5 50.8 %collective-permute-start = (f32[4,64,512]{2,1,0:T(8,128)}, f32[4,64,512]{2,1,0:T(8,128)}, u32[]{:S(2)}, u32[]{:S(2)}) collective-permute-start(f32[4,64,512]{2,1,0:T(8,128)} %get-tuple-element.58), channel_id=1, source_target_pairs={{1,0},{2,1},{3,2},{4,3},{5,4},{6,5},{7,6},{9,8},{10,9},{11,10},{12... | collective-permute-start | bytes 1572872 | tf_op jit(solution)/shard_map/ppermute | solution.py:22
  10.8 49.5 %collective-permute-start.1 = (f32[4,64,512]{2,1,0:T(8,128)}, f32[4,64,512]{2,1,0:T(8,128)}, u32[]{:S(2)}, u32[]{:S(2)}) collective-permute-start(f32[4,64,512]{2,1,0:T(8,128)} %get-tuple-element.59), channel_id=1, source_target_pairs={{0,1},{1,2},{2,3},{3,4},{4,5},{5,6},{6,7},{8,9},{9,10},{10,11},{11... | collective-permute-start | bytes 1572872 | tf_op jit(solution)/shard_map/ppermute | solution.py:19
  17.1 3.3 %copy-start.11 = (s32[1,6,16,64,128]{4,3,2,1,0:T(8,128)S(1)}, s32[1,6,16,64,128]{4,3,2,1,0:T(8,128)}, u32[]{:S(2)}) copy-start(s32[1,6,16,64,128]{4,3,2,1,0:T(8,128)} %param.14) | copy-start | bytes 9437188
  20.4 3.7 %copy-start.24 = (s32[1,256]{1,0:T(1,128)S(1)}, s32[1,256]{1,0:T(1,128)}, u32[]{:S(2)}) copy-start(s32[1,256]{1,0:T(1,128)} %param.17) | copy-start | bytes 3076
  20.4 3.7 %copy-start.21 = (s32[1,6,16,256]{3,2,1,0:T(8,128)S(1)}, s32[1,6,16,256]{3,2,1,0:T(8,128)}, u32[]{:S(2)}) copy-start(s32[1,6,16,256]{3,2,1,0:T(8,128)} %param.15) | copy-start | bytes 294916
  20.4 3.8 %copy-start.25 = (f32[64]{0:T(128)S(1)}, f32[64]{0:T(128)}, u32[]{:S(2)}) copy-start(f32[64]{0:T(128)} %param.16) | copy-start | bytes 772
  30.3 2.8 copy-start.8
  30.3 2.8 copy-start.9
  33.1 2.8 copy-start.12
  33.1 2.8 copy-start.13
  33.1 2.8 copy-start.14
  33.1 2.8 copy-start.15
  33.1 2.8 copy-start.16
  33.1 2.8 copy-start.17
  33.2 2.8 copy-start.18
  33.2 2.8 copy-start.19
  38.6 9.6 %copy-start.10 = (f32[16,64,4,128]{3,1,0,2:T(8,128)}, f32[16,64,4,128]{3,1,0,2:T(8,128)S(1)}, u32[]{:S(2)}) copy-start(f32[16,64,4,128]{3,1,0,2:T(8,128)S(1)} %get-tuple-element.83) | copy-start | bytes 6291460
  51.7 8.0 %copy-start.23 = (f32[1,4,256]{2,1,0:T(4,128)S(1)}, f32[1,4,256]{2,1,0:T(4,128)}, u32[]{:S(2)}) copy-start(f32[1,4,256]{2,1,0:T(4,128)} %param.18) | copy-start | bytes 12292
  51.7 8.6 %copy-start.2 = (f32[16,64,512]{2,1,0:T(8,128)S(1)}, f32[16,64,512]{2,1,0:T(8,128)}, u32[]{:S(2)}) copy-start(f32[16,64,512]{2,1,0:T(8,128)} %param.13) | copy-start | bytes 6291460
  93.1 9.8 %copy-start.7 = (f32[524288]{0:T(1024)}, f32[524288]{0:T(1024)S(1)}, u32[]{:S(2)}) copy-start(f32[524288]{0:T(1024)S(1)} %scatter_fusion) | copy-start | bytes 6291460
  96.1 26.2 %collective-permute-start.3 = (f32[4,64,512]{2,1,0:T(8,128)}, f32[4,64,512]{2,1,0:T(8,128)}, u32[]{:S(2)}, u32[]{:S(2)}) collective-permute-start(f32[4,64,512]{2,1,0:T(8,128)} %slice.517), channel_id=1, source_target_pairs={{0,1},{1,2},{2,3},{3,4},{4,5},{5,6},{6,7},{8,9},{9,10},{10,11},{11... | collective-permute-start | bytes 1572872 | tf_op jit(solution)/shard_map/ppermute | solution.py:19
  102.9 21.1 %collective-permute-start.2 = (f32[4,64,512]{2,1,0:T(8,128)}, f32[4,64,512]{2,1,0:T(8,128)}, u32[]{:S(2)}, u32[]{:S(2)}) collective-permute-start(f32[4,64,512]{2,1,0:T(8,128)} %slice.514), channel_id=1, source_target_pairs={{1,0},{2,1},{3,2},{4,3},{5,4},{6,5},{7,6},{9,8},{10,9},{11,10},{12... | collective-permute-start | bytes 1572872 | tf_op jit(solution)/shard_map/ppermute | solution.py:22
  123.4 2.4 copy-start.6
  137.3 9.7 %copy-start.22 = (s32[1,3]{1,0:T(1,128)S(1)}, s32[1,3]{1,0:T(1,128)}, u32[]{:S(2)}) copy-start(s32[1,3]{1,0:T(1,128)} %param.19) | copy-start | bytes 40
  141.5 25.7 %collective-permute-start.5 = (f32[4,64,512]{2,1,0:T(8,128)}, f32[4,64,512]{2,1,0:T(8,128)}, u32[]{:S(2)}, u32[]{:S(2)}) collective-permute-start(f32[4,64,512]{2,1,0:T(8,128)} %slice.548), channel_id=1, source_target_pairs={{0,1},{1,2},{2,3},{3,4},{4,5},{5,6},{6,7},{8,9},{9,10},{10,11},{11... | collective-permute-start | bytes 1572872 | tf_op jit(solution)/shard_map/ppermute | solution.py:19
  150.2 20.3 %collective-permute-start.4 = (f32[4,64,512]{2,1,0:T(8,128)}, f32[4,64,512]{2,1,0:T(8,128)}, u32[]{:S(2)}, u32[]{:S(2)}) collective-permute-start(f32[4,64,512]{2,1,0:T(8,128)} %slice.545), channel_id=1, source_target_pairs={{1,0},{2,1},{3,2},{4,3},{5,4},{6,5},{7,6},{9,8},{10,9},{11,10},{12... | collective-permute-start | bytes 1572872 | tf_op jit(solution)/shard_map/ppermute | solution.py:22
  168.2 3.4 %copy-start = (f32[16,64,512]{2,1,0:T(8,128)S(1)}, f32[16,64,512]{2,1,0:T(8,128)}, u32[]{:S(2)}) copy-start(f32[16,64,512]{2,1,0:T(8,128)} %reshape.605) | copy-start | bytes 6291460
  168.2 3.4 %copy-start.4 = (f32[16,64,512]{2,1,0:T(8,128)S(1)}, f32[16,64,512]{2,1,0:T(8,128)}, u32[]{:S(2)}) copy-start(f32[16,64,512]{2,1,0:T(8,128)} %param.13) | copy-start | bytes 6291460
  187.4 13.6 %collective-permute-start.7 = (f32[4,64,512]{2,1,0:T(8,128)}, f32[4,64,512]{2,1,0:T(8,128)}, u32[]{:S(2)}, u32[]{:S(2)}) collective-permute-start(f32[4,64,512]{2,1,0:T(8,128)} %slice.582), channel_id=1, source_target_pairs={{0,1},{1,2},{2,3},{3,4},{4,5},{5,6},{6,7},{8,9},{9,10},{10,11},{11... | collective-permute-start | bytes 1572872 | tf_op jit(solution)/shard_map/ppermute | solution.py:19
  214.3 54.2 %collective-permute-start.6 = (f32[4,64,512]{2,1,0:T(8,128)S(1)}, f32[4,64,512]{2,1,0:T(8,128)S(1)}, u32[]{:S(2)}, u32[]{:S(2)}) collective-permute-start(f32[4,64,512]{2,1,0:T(8,128)S(1)} %slice.579), channel_id=1, source_target_pairs={{1,0},{2,1},{3,2},{4,3},{5,4},{6,5},{7,6},{9,8},{10,9},{11,10},{12... | collective-permute-start | bytes 1572872 | tf_op jit(solution)/shard_map/ppermute | solution.py:22
  265.6 3.7 %copy-start.1 = (f32[16,64,512]{2,1,0:T(8,128)S(1)}, f32[16,64,512]{2,1,0:T(8,128)}, u32[]{:S(2)}) copy-start(f32[16,64,512]{2,1,0:T(8,128)} %reshape.605) | copy-start | bytes 6291460
  (3 other events, 4.5 us)
Sparse Core Ops, SparseCore 0:
  213.4 33.5 reduce-scatter.1
where the time goes:
time: 310 us; the launch traced here: 308 us
  other arithmetic  113 us (36%)
  local copies, waits for them, and re-layouts  74.6 us (24%)
  blocking collectives  46.7 us (15%)
  waiting for transfers between devices  28.4 us (9%)
  starting transfers between devices  26.9 us (9%)
  between operations  18.8 us (6%)
    add x4, other arithmetic, body(): stepped = 2.0 * now - later + courant * laplace(now)  65.4 us
    psum x1, blocking collectives, body(): misfit = 0.5 * lax.psum(misfit_part, ('shot', 'space')) / count  46.7 us
    ppermute x4, waiting for transfers between devices, with_halo(): lax.ppermute(lax.slice_in_dim(block, block.shape[dim] - width, None, axis...  28.3 us
    ppermute x4, starting transfers between devices, with_halo(): lax.ppermute(lax.slice_in_dim(block, block.shape[dim] - width, None, axis...  21.5 us
    scatter-add x4, other arithmetic, body(): stepped.reshape(-1).at[cells].add(residual).reshape(depth, rows, cols)  15.3 us
    unnamed x2, other arithmetic  14.8 us
    unnamed x61, local copies, waits for them, and re-layouts  13.9 us
    gather x4, local copies, waits for them, and re-layouts, body(): synthetic = jnp.take(fields[level].reshape(-1), cells)  13.8 us
  transfers between devices with their start and end apart: 9, of which 3 were waited for; matrix products, arithmetic and copies ran while one was open for 33% of the time, Pallas kernels for 0%

commit v1 on v0

v1 whole, which is shorter than its diff:
```python
import functools

import jax
import jax.numpy as jnp
from jax import lax
from jax.experimental import pallas as pl
from jax.experimental.pallas import tpu as pltpu
from jax.sharding import PartitionSpec as P

ITERS = 4
MUTE = 8
LANES = 128
SUB = 8
REACH = 4

COEFFS = (-205.0 / 72.0, 8.0 / 5.0, -1.0 / 5.0, 8.0 / 315.0, -1.0 / 560.0)

VMEM = pl.BlockSpec(memory_space=pltpu.VMEM)
SMEM = pl.BlockSpec(memory_space=pltpu.SMEM)
ANY = pl.BlockSpec(memory_space=pl.ANY)


def params(mib):
    return pltpu.CompilerParams(vmem_limit_bytes=mib * 1024 * 1024)


def cost(us):
    return pl.CostEstimate(flops=int(us * 5e6), bytes_accessed=0, transcendentals=0)


def quotient(value, by):
    if by & (by - 1) == 0:
        return jnp.right_shift(value, by.bit_length() - 1)
    return value // by


def stack_planes(source, first, count, ypad):
    _, rows, cols = source.shape
    zero = jnp.zeros((SUB, LANES), jnp.float32)

    def step(j, carry):
        for t in range(cols // LANES):
            ypad[j, t, 0:SUB, :] = zero
            ypad[j, t, SUB + rows : 2 * SUB + rows, :] = zero
            ypad[j, t, SUB : SUB + rows, :] = source[first + j, :, t * LANES : (t + 1) * LANES]
        return carry

    lax.fori_loop(0, count, step, 0)


def update_planes(count, ypad, column, column_first, place, later, courant, added, new):
    _, rows, cols = new.shape
    tiles = cols // LANES
    lane = lax.broadcasted_iota(jnp.int32, (SUB, LANES), 1)
    zero = jnp.zeros((SUB, LANES), jnp.float32)

    def plane(j, carry):
        z = place + j
        for r in range(rows // SUB):
            y = slice(r * SUB, (r + 1) * SUB)
            centre = [ypad[j, t, SUB + r * SUB : 2 * SUB + r * SUB, :] for t in range(tiles)]
            total = [3.0 * COEFFS[0] * c for c in centre]
            for i in range(1, REACH + 1):
                right = [pltpu.roll(c, i, 1) for c in centre]
                left = [pltpu.roll(c, LANES - i, 1) for c in centre]
                for t in range(tiles):
                    x = slice(t * LANES, (t + 1) * LANES)
                    before = jnp.where(lane < i, right[t - 1] if t else zero, right[t])
                    after = jnp.where(
                        lane >= LANES - i, left[t + 1] if t + 1 < tiles else zero, left[t]
                    )
                    near = ypad[j, t, SUB + r * SUB - i : 2 * SUB + r * SUB - i, :]
                    far = ypad[j, t, SUB + r * SUB + i : 2 * SUB + r * SUB + i, :]
                    below = column[column_first + j - i, y, x]
                    above = column[column_first + j + i, y, x]
                    total[t] = total[t] + COEFFS[i] * (
                        ((before + after) + (near + far)) + (below + above)
                    )
            for t in range(tiles):
                x = slice(t * LANES, (t + 1) * LANES)
                value = (2.0 * centre[t] - later[z, y, x]) + (
                    courant[z, y, x] * total[t] + added[z, y, x]
                )
                new[j, y, x] = value
        return carry

    lax.fori_loop(0, count, plane, 0)


def inner_kernel(now, later, courant, added, new, ypad):
    depth = now.shape[0]
    count = depth - 2 * REACH
    stack_planes(now, REACH, count, ypad)
    update_planes(count, ypad, now, REACH, REACH, later, courant, added, new)


def edge(place, now, halo, later, courant, added, strip, ypad, column):
    depth, rows, cols = now.shape
    first = place[0]
    high = first > 0
    halo_at = jnp.where(high, 2 * REACH, 0)
    own_at = jnp.where(high, 0, REACH)
    own_first = jnp.where(high, depth - 2 * REACH, 0)

    def copy_halo(j, carry):
        column[halo_at + j] = halo[j]
        return carry

    def copy_own(j, carry):
        column[own_at + j] = now[own_first + j]
        return carry

    lax.fori_loop(0, REACH, copy_halo, 0)
    lax.fori_loop(0, 2 * REACH, copy_own, 0)
    stack_planes(now, first, REACH, ypad)
    update_planes(REACH, ypad, column, REACH, first, later, courant, added, strip)


def pair_kernel(place, now, halo, later, courant, added, strip, ypad, column):
    edge(place, now, halo, later, courant, added, strip, ypad, column)


def cross_kernel(
    place, now, halo, later, courant, added, middle, other, new, strip, ypad, column
):
    depth = now.shape[0]
    edge(place, now, halo, later, courant, added, strip, ypad, column)
    first = place[0]
    opposite = depth - REACH - first

    def copy_edges(j, carry):
        new[first + j] = strip[j]
        new[opposite + j] = other[j]
        return carry

    def copy_middle(j, carry):
        new[REACH + j] = middle[j]
        return carry

    lax.fori_loop(0, REACH, copy_edges, 0)
    lax.fori_loop(0, depth - 2 * REACH, copy_middle, 0)


def source_kernel(
    first, cell, codes, index, table, observed, *refs
):
    spread = refs[:ITERS]
    squares = refs[ITERS]
    packed, onehot = refs[ITERS + 1 :]
    _, depth, rows, words = codes.shape
    cols = spread[0].shape[2]
    tiles = cols // LANES
    count = cell.shape[1]
    flat = cell[...] - first[0]
    zy = quotient(flat, cols)
    x = flat - zy * cols
    z = quotient(zy, rows)
    block = (zy - z * rows) * tiles + quotient(x, LANES)
    packed[...] = jnp.zeros(packed.shape, jnp.float32)
    for k, line in enumerate((x, zy, z, block)):
        packed[k : k + 1, :] = line.astype(jnp.float32)
    packed[SUB : SUB + ITERS, :] = observed[...]
    turned = jnp.concatenate(
        [packed[:, k * LANES : (k + 1) * LANES].T for k in range(count // LANES)], axis=0
    )
    x_col, zy_col, z_col, block_col = (turned[:, k : k + 1].astype(jnp.int32) for k in range(4))
    one = jnp.ones((), jnp.float32)
    none = jnp.zeros((), jnp.float32)

    def hot(shape, col):
        return jnp.where(lax.broadcasted_iota(jnp.int32, shape, 1) == col, one, none)

    onehot[...] = hot((count, depth * rows), zy_col).astype(jnp.bfloat16)
    at_z = hot((count, depth), z_col).astype(jnp.bfloat16)
    at_x = lax.broadcasted_iota(jnp.int32, (count, cols), 1) == x_col
    at_block = lax.broadcasted_iota(jnp.int32, (count, rows * tiles), 1) == block_col
    total = jnp.zeros((count, 1), jnp.float32)
    parts = []
    for step in range(ITERS):
        level = ITERS - step
        word = codes[level].reshape(depth * rows, words)
        code = jnp.concatenate(
            [
                (jnp.bitwise_and(jnp.right_shift(word, 8 * m), 255) - 128)
                .astype(jnp.float32)
                .astype(jnp.bfloat16)
                for m in range(tiles)
            ],
            axis=1,
        )
        lines = jnp.dot(onehot[...], code, preferred_element_type=jnp.float32)
        picked = jnp.sum(jnp.where(at_x, lines, 0.0), axis=1, keepdims=True)
        entries = jnp.dot(
            at_z,
            index[level].astype(jnp.float32).astype(jnp.bfloat16),
            preferred_element_type=jnp.float32,
        )
        entry = jnp.sum(jnp.where(at_block, entries, 0.0), axis=1, keepdims=True)
        at_entry = lax.broadcasted_iota(jnp.int32, (count, LANES), 1) == entry.astype(jnp.int32)
        scale = jnp.sum(jnp.where(at_entry, table[...], 0.0), axis=1, keepdims=True)
        residual = picked * scale - turned[:, SUB + level - 1 : SUB + level]
        total = total + residual * residual
        dense = jnp.where(at_x, residual, 0.0)
        head = dense.astype(jnp.bfloat16)
        rest = dense - head.astype(jnp.float32)
        middle = rest.astype(jnp.bfloat16)
        tail = (rest - middle.astype(jnp.float32)).astype(jnp.bfloat16)
        parts.append((head, middle, tail))
    squares[...] = jnp.broadcast_to(jnp.sum(total, axis=0, keepdims=True), squares.shape)

    group = 4

    for step in range(ITERS):
        pieces = parts[step]

        def planes(k, carry, out=spread[step], pieces=pieces):
            rank = lax.broadcasted_iota(jnp.int32, (group * rows, count), 0) + k * (group * rows)
            at = jnp.where(rank == zy, one, none).astype(jnp.bfloat16)
            value = sum(
                jnp.dot(at, piece, preferred_element_type=jnp.float32) for piece in pieces
            )
            out[pl.ds(k * group, group)] = value.reshape(group, rows, cols)
            return carry

        lax.fori_loop(0, depth // group, planes, 0)


def image_kernel(
    place, codes, index, table, w0, w1, w2, image, last, packed, turned, ey
):
    levels, depth, rows, words = codes.shape
    cols = image.shape[2]
    tiles = cols // LANES
    first_z, source_z, source_y, source_x = (place[k] for k in range(4))
    scale_by = -1.0 / (2.0 * MUTE * MUTE)
    lane = lax.broadcasted_iota(jnp.int32, (SUB, LANES), 1)

    def bell(distance):
        off = distance.astype(jnp.float32)
        return jnp.exp(off * off * scale_by)

    packed[...] = jnp.zeros(packed.shape, jnp.float32)
    lines = levels * depth
    chosen = index[...].reshape(lines, rows * tiles)
    across = jnp.broadcast_to(table[...], (lines, LANES))
    for h in range(rows * tiles // LANES):
        cut = slice(h * LANES, (h + 1) * LANES)
        packed[0:lines, cut] = jnp.take_along_axis(
            across, chosen[:, cut], axis=1, mode="promise_in_bounds"
        )
        turned[cut, :] = packed[:, cut].T
    ey[...] = bell(lax.broadcasted_iota(jnp.int32, (rows, LANES), 0) - source_y)
    ex = [bell(lane + (t * LANES) - source_x) for t in range(tiles)]

    def plane(z, carry):
        ez = bell(jnp.full((SUB, LANES), first_z + z - source_z, jnp.int32))
        for r in range(rows // SUB):
            y = slice(r * SUB, (r + 1) * SUB)
            word = [codes[level, z, y, :] for level in range(levels)]
            down = ez * ey[y, :]
            for t in range(tiles):
                x = slice(t * LANES, (t + 1) * LANES)
                scales = pltpu.roll(
                    turned[pl.ds(t + tiles * SUB * r, SUB, stride=tiles), :],
                    lax.rem(LANES - z, LANES),
                    1,
                )
                field = []
                for level in range(levels):
                    code = jnp.bitwise_and(jnp.right_shift(word[level], 8 * t), 255) - 128
                    scale = jnp.broadcast_to(
                        scales[:, level * depth : level * depth + 1], (SUB, LANES)
                    )
                    field.append(code.astype(jnp.float32) * scale)
                bend = [
                    None if k in (0, levels - 1)
                    else (field[k + 1] - 2.0 * field[k]) + field[k - 1]
                    for k in range(levels)
                ]
                mute = 1.0 - down * ex[t]
                value = w0[z, y, x] * bend[ITERS]
                value = value + w1[z, y, x] * bend[ITERS - 1]
                value = value + w2[z, y, x] * bend[ITERS - 2]
                image[z, y, x] = mute * value
                last[z, y, x] = mute * bend[ITERS - 3]
        return carry

    lax.fori_loop(0, depth, plane, 0)


def split_kernel(side, image, last, w3, kept, sent):
    half, depth, block, cols = kept.shape
    mine = side[0]

    def plane(z, carry):
        for q in range(half):
            for out, which in ((kept, mine), (sent, 1 - mine)):
                y = pl.ds(pl.multiple_of((2 * q + which) * block, SUB), block)
                out[q, z] = image[z, y, :] + last[z, y, :] * w3[z, y, :]
        return carry

    lax.fori_loop(0, depth, plane, 0)


def summed(value, axis):
    count = lax.axis_size(axis)
    if count & (count - 1):
        return lax.psum(value, axis)
    hop = 1
    while hop < count:
        value = value + lax.ppermute(value, axis, [(i, i ^ hop) for i in range(count)])
        hop *= 2
    return value


def body(
    adjoint_now,
    adjoint_later,
    courant,
    checkpoint_codes,
    scale_index,
    scale_table,
    receiver_cell,
    observed,
    source_cell,
):
    now = adjoint_now[0]
    later = adjoint_later[0]
    codes = checkpoint_codes[0]
    index = scale_index[0]
    depth, rows, cols = now.shape
    levels = codes.shape[0]
    tiles = cols // LANES
    receivers = receiver_cell.shape[1]
    slabs = lax.axis_size("space")
    shots = lax.axis_size("shot")
    slab = lax.axis_index("space")
    shot = lax.axis_index("shot")
    even = slab % 2 == 0
    pair_place = jnp.where(even, depth - REACH, 0).astype(jnp.int32)
    cross_place = (depth - REACH) - pair_place
    pairs = [(i, i ^ 1) for i in range(slabs) if i ^ 1 < slabs]
    crosses = [(i, i + 1) for i in range(1, slabs - 1, 2)]
    crosses = crosses + [(b, a) for a, b in crosses]
    field = jax.ShapeDtypeStruct((depth, rows, cols), jnp.float32)
    strip = jax.ShapeDtypeStruct((REACH, rows, cols), jnp.float32)
    first_z = slab * depth

    def pair_exchange(block):
        return lax.ppermute(block, "space", pairs)

    def cross_exchange(block):
        return lax.ppermute(block, "space", crosses)

    ypad = (tiles, rows + 2 * SUB, LANES)
    middle = jax.ShapeDtypeStruct((depth - 2 * REACH, rows, cols), jnp.float32)
    edge_scratch = [
        pltpu.VMEM((REACH,) + ypad, jnp.float32),
        pltpu.VMEM((3 * REACH, rows, cols), jnp.float32),
    ]
    inner = pl.pallas_call(
        inner_kernel,
        out_shape=middle,
        in_specs=[VMEM] * 4,
        out_specs=VMEM,
        scratch_shapes=[pltpu.VMEM((depth - 2 * REACH,) + ypad, jnp.float32)],
        compiler_params=params(20),
        cost_estimate=cost(3),
        name="inner",
    )
    pair = pl.pallas_call(
        pair_kernel,
        out_shape=strip,
        in_specs=[SMEM] + [VMEM] * 5,
        out_specs=VMEM,
        scratch_shapes=edge_scratch,
        compiler_params=params(20),
        cost_estimate=cost(2),
        name="pair",
    )
    cross = pl.pallas_call(
        cross_kernel,
        out_shape=(field, strip),
        in_specs=[SMEM] + [VMEM] * 7,
        out_specs=(VMEM, VMEM),
        scratch_shapes=edge_scratch,
        compiler_params=params(20),
        cost_estimate=cost(2),
        name="cross",
    )

    pair_halo = pair_exchange(lax.dynamic_slice_in_dim(now, pair_place, REACH, 0))
    cross_halo = cross_exchange(lax.dynamic_slice_in_dim(now, cross_place, REACH, 0))

    table = jnp.pad(scale_table, (0, LANES - scale_table.shape[0])).reshape(1, LANES)
    *added, squares = pl.pallas_call(
        source_kernel,
        out_shape=[field] * ITERS + [jax.ShapeDtypeStruct((SUB, LANES), jnp.float32)],
        in_specs=[SMEM] + [VMEM] * 5,
        out_specs=[VMEM] * (ITERS + 1),
        scratch_shapes=[
            pltpu.VMEM((LANES, receivers), jnp.float32),
            pltpu.VMEM((receivers, depth * rows), jnp.bfloat16),
        ],
        compiler_params=params(28),
        cost_estimate=cost(8),
        name="sources",
    )(
        (first_z * (rows * cols)).reshape(1).astype(jnp.int32),
        receiver_cell,
        codes,
        index,
        table,
        observed[0],
    )

    waves = [now]
    for step in range(ITERS):
        now = waves[-1]
        within = inner(now, later, courant, added[step])
        pair_sent = pair(pair_place.reshape(1), now, pair_halo, later, courant, added[step])
        if step + 1 < ITERS:
            pair_halo = pair_exchange(pair_sent)
        new, cross_sent = cross(
            cross_place.reshape(1),
            now,
            cross_halo,
            later,
            courant,
            added[step],
            within,
            pair_sent,
        )
        if step + 1 < ITERS:
            cross_halo = cross_exchange(cross_sent)
        later = now
        waves.append(new)

    place = jnp.concatenate([first_z.reshape(1).astype(jnp.int32), source_cell[0]])
    image, last = pl.pallas_call(
        image_kernel,
        out_shape=(field, field),
        in_specs=[SMEM] + [VMEM] * 6,
        out_specs=(VMEM, VMEM),
        scratch_shapes=[
            pltpu.VMEM((LANES, rows * tiles), jnp.float32),
            pltpu.VMEM((rows * tiles, LANES), jnp.float32),
            pltpu.VMEM((rows, LANES), jnp.float32),
        ],
        compiler_params=params(28),
        cost_estimate=cost(5),
        name="image",
    )(place, codes, index, table, waves[0], waves[1], waves[2])

    block = rows // shots
    part = jax.ShapeDtypeStruct((shots // 2, depth, block, cols), jnp.float32)
    kept, sent = pl.pallas_call(
        split_kernel,
        out_shape=(part, part),
        in_specs=[SMEM] + [VMEM] * 3,
        out_specs=(VMEM, VMEM),
        compiler_params=params(20),
        cost_estimate=cost(2),
        name="split",
    )((shot % 2).reshape(1).astype(jnp.int32), image, last, waves[3])
    hop = 1
    while True:
        kept = kept + lax.ppermute(sent, "shot", [(i, i ^ hop) for i in range(shots)])
        hop *= 2
        if hop >= shots:
            break
        mine = (shot // hop) % 2
        halves = kept.reshape((kept.shape[0] // 2, 2) + kept.shape[1:])
        kept = lax.dynamic_index_in_dim(halves, mine, 1, keepdims=False)
        sent = lax.dynamic_index_in_dim(halves, 1 - mine, 1, keepdims=False)
    gradient = kept[0]

    squares = summed(summed(squares, "space"), "shot")
    misfit = 0.5 * squares[0, 0] / (shots * ITERS * receivers * slabs)
    return (gradient, waves[4][None], waves[3][None], misfit)


def solution(mesh):
    placed = (
        P("shot", "space", None, None),
        P("shot", "space", None, None),
        P("space", None, None),
        P("shot", None, "space", None, None),
        P("shot", None, "space", None),
        P(),
        P("shot", "space"),
        P("shot", None, "space"),
        P("shot", None),
    )
    return jax.shard_map(
        body,
        mesh=mesh,
        in_specs=placed,
        out_specs=(
            P("space", "shot", None),
            P("shot", "space", None, None),
            P("shot", "space", None, None),
            P(),
        ),
        check_vma=False,
    )
```

time: 310 us -> 161 us (0.52)
  other arithmetic: 113 us -> 3.8 us
  Pallas kernels: 0 us -> 60.8 us
  local copies, waits for them, and re-layouts: 74.6 us -> 24.8 us
  blocking collectives: 46.7 us -> 0 us
  between operations: 18.8 us -> 2.81 us
  waiting for transfers between devices: 28.4 us -> 40.9 us
    add x5 -> x6, other arithmetic: 65.5 us -> 1.77 us  [the longest x1 1.76 us: body(): kept + lax.ppermute(sent, 'shot', [(i, i ^ hop) for i in range(shots)])]
    pallas_call x0 -> x15, Pallas kernels: none -> 60.8 us  [the longest x1 19.6 us: body(): pl.pallas_call(image_kernel, out_shape=(field, field), in_specs=[SMEM] +...]
    psum x1 -> x0, blocking collectives: 46.7 us -> none  [body(): misfit = 0.5 * lax.psum(misfit_part, ('shot', 'space')) / count]
    slice x12 -> x1, local copies, waits for them, and re-layouts: 18.2 us -> 0.51 us  [body(): misfit = 0.5 * squares[0, 0] / (shots * ITERS * receivers * slabs)]
    scatter-add x4 -> x0, other arithmetic: 15.3 us -> none  [body(): stepped.reshape(-1).at[cells].add(residual).reshape(depth, rows, cols)]
    unnamed x2 -> x0, other arithmetic: 14.8 us -> none
    gather x4 -> x0, local copies, waits for them, and re-layouts: 13.8 us -> none  [body(): synthetic = jnp.take(fields[level].reshape(-1), cells)]
    mul x10 -> x0, local copies, waits for them, and re-layouts: 13.2 us -> none  [decode(): centred.reshape(depth, rows, cols // QBLOCK, QBLOCK)]
  transfers between devices with their start and end apart: 9 -> 15, of which waited for: 3 -> 7; matrix products, arithmetic and copies ran while one was open for 33% -> 2% of each run, Pallas kernels for 0% -> 35%
where the time goes in v1:
time: 161 us; the launch traced here: 160 us
  Pallas kernels  60.8 us (38%)
  waiting for transfers between devices  40.9 us (25%)
  starting transfers between devices  26.8 us (17%)
  local copies, waits for them, and re-layouts  24.8 us (15%)
  other arithmetic  3.8 us (2%)
  between operations  2.81 us (2%)
    ppermute x5, waiting for transfers between devices, summed(): lax.ppermute(value, axis, [(i, i ^ hop) for i in range(count)])  21.2 us
    unnamed x58, local copies, waits for them, and re-layouts  21.1 us
    ppermute x4, waiting for transfers between devices, pair_exchange(): return lax.ppermute(block, 'space', pairs)  19.7 us
    pallas_call x1, Pallas kernels, body(): pl.pallas_call(image_kernel, out_shape=(field, field), in_specs=[SMEM] +...  19.6 us
    pallas_call x4, Pallas kernels, body(): cross(cross_place.reshape(1), now, cross_halo, later, courant, added[step...  12.8 us
    pallas_call x4, Pallas kernels, body(): within = inner(now, later, courant, added[step])  11.8 us
    ppermute x4, starting transfers between devices, pair_exchange(): return lax.ppermute(block, 'space', pairs)  11.5 us
    ppermute x5, starting transfers between devices, summed(): lax.ppermute(value, axis, [(i, i ^ hop) for i in range(count)])  9.49 us
  transfers between devices with their start and end apart: 15, of which 7 were waited for; matrix products, arithmetic and copies ran while one was open for 2% of the time, Pallas kernels for 35%

profile of v1, /device:TPU:0, one launch (start us, length us, event | category | flops | bytes accessed | tf_op | source)
XLA Modules:
  0.0 159.8 jit_solution(5011749478643601832)
XLA Ops:
  0.7 2.3 %dynamic-slice_bitcast_fusion = (f32[4,64,512]{2,1,0:T(8,128)}, f32[4,64,512]{2,1,0:T(8,128)}) fusion(f32[1,16,64,512]{3,2,1,0:T(8,128)} %param.9, s32[]{:T(128)} %select_n.36, s32[]{:T(128)S(6)} %select_n.37), kind=kLoop, calls=%fused_computation.1 | loop fusion | bytes 2097160 | tf_op jit(solution)/shard_map/dynamic_slice | solution.py:392
  3.0 3.0 %collective-permute-start.1 = (f32[4,64,512]{2,1,0:T(8,128)}, f32[4,64,512]{2,1,0:T(8,128)S(1)}, u32[]{:S(2)}, u32[]{:S(2)}) collective-permute-start(f32[4,64,512]{2,1,0:T(8,128)} %get-tuple-element.36), channel_id=1, source_target_pairs={{0,1},{1,0},{2,3},{3,2},{4,5},{5,4},{6,7},{7,6},{8,9},{9,8},{10,11... | collective-permute-start | bytes 1572872 | tf_op jit(solution)/shard_map/ppermute | solution.py:350
  6.7 1.9 %copy-done.18 = s32[1,6,16,64,128]{4,3,2,1,0:T(8,128)S(1)} copy-done((s32[1,6,16,64,128]{4,3,2,1,0:T(8,128)S(1)}, s32[1,6,16,64,128]{4,3,2,1,0:T(8,128)}, u32[]{:S(2)}) %copy-start.18) | copy-done | bytes 3145752
  8.6 8.9 %sources.1 = (f32[16,64,512]{2,1,0:T(8,128)S(1)}, f32[16,64,512]{2,1,0:T(8,128)S(1)}, f32[16,64,512]{2,1,0:T(8,128)S(1)}, f32[16,64,512]{2,1,0:T(8,128)S(1)}, f32[8,128]{1,0:T(8,128)S(1)}) custom-call(s32[1]{0:T(128)} %bitcast.10.first, s32[1,256]{1,0:T(1,128)S(1)} %copy-done.23, s32[6,16,64,128]{3,2,1,0:T(8,128)S(1)} %bitcast.33, ...), custom_call_target="tpu_custom_call" | custom-call | flops 40000000 | tf_op jit(solution)/shard_map/sources/pallas_call | solution.py:396
  17.5 3.1 %copy-done.1 = f32[1,16,64,512]{3,2,1,0:T(8,128)S(1)} copy-done((f32[1,16,64,512]{3,2,1,0:T(8,128)S(1)}, f32[1,16,64,512]{3,2,1,0:T(8,128)}, u32[]{:S(2)}) %copy-start.1) | copy-done | bytes 2097176
  20.6 1.6 copy-done.12
  22.1 3.0 %inner.4.middle = f32[8,64,512]{2,1,0:T(8,128)S(1)} custom-call(f32[16,64,512]{2,1,0:T(8,128)S(1)} %bitcast.22, f32[16,64,512]{2,1,0:T(8,128)S(1)} %bitcast.30, f32[16,64,512]{2,1,0:T(8,128)S(1)} %copy-done, f32[16,64,512]{2,1,0:T(8,128)S(1)} %get-tuple-element.20.added), custom_call_target="tpu_custom_call" | custom-call | flops 15000000 | tf_op jit(solution)/shard_map/inner/pallas_call | solution.py:420
  25.1 3.5 %collective-permute-done.1.halo = f32[4,64,512]{2,1,0:T(8,128)S(1)} collective-permute-done((f32[4,64,512]{2,1,0:T(8,128)}, f32[4,64,512]{2,1,0:T(8,128)S(1)}, u32[]{:S(2)}, u32[]{:S(2)}) %collective-permute-start.1) | collective-permute-done | bytes 524320 | tf_op jit(solution)/shard_map/ppermute | solution.py:350
  30.3 2.4 %collective-permute-start.3 = (f32[4,64,512]{2,1,0:T(8,128)S(1)}, f32[4,64,512]{2,1,0:T(8,128)S(1)}, u32[]{:S(2)}, u32[]{:S(2)}) collective-permute-start(f32[4,64,512]{2,1,0:T(8,128)S(1)} %pair.4.other), channel_id=1, source_target_pairs={{0,1},{1,0},{2,3},{3,2},{4,5},{5,4},{6,7},{7,6},{8,9},{9,8},{10,11... | collective-permute-start | bytes 1572872 | tf_op jit(solution)/shard_map/ppermute | solution.py:350
  32.7 1.7 %cross.4 = (f32[16,64,512]{2,1,0:T(8,128)S(1)}, f32[4,64,512]{2,1,0:T(8,128)S(1)}) custom-call(s32[1]{0:T(128)} %bitcast.7.place, f32[16,64,512]{2,1,0:T(8,128)S(1)} %bitcast.24, f32[4,64,512]{2,1,0:T(8,128)S(1)} %collective-permute-done.halo, f32[16,64,512]{2,1,0:T(8,128)S(1)} %bitcast.32, f32[16,64,512]{2,1,0:T(8,128)S(1)} %copy-done, ...), custom_call_target="tpu_custom_call" | custom-call | flops 10000000 | tf_op jit(solution)/shard_map/cross/pallas_call | solution.py:424
  35.2 3.0 %inner.5.middle = f32[8,64,512]{2,1,0:T(8,128)S(1)} custom-call(f32[16,64,512]{2,1,0:T(8,128)S(1)} %get-tuple-element.21.now.w1.later, f32[16,64,512]{2,1,0:T(8,128)S(1)} %bitcast.25, f32[16,64,512]{2,1,0:T(8,128)S(1)} %copy-done, f32[16,64,512]{2,1,0:T(8,128)S(1)} %get-tuple-element.23.added), custom_call_target="tpu_custom_call" | custom-call | flops 15000000 | tf_op jit(solution)/shard_map/inner/pallas_call | solution.py:420
  38.1 16.1 %collective-permute-done.3.halo = f32[4,64,512]{2,1,0:T(8,128)S(1)} collective-permute-done((f32[4,64,512]{2,1,0:T(8,128)S(1)}, f32[4,64,512]{2,1,0:T(8,128)S(1)}, u32[]{:S(2)}, u32[]{:S(2)}) %collective-permute-start.3) | collective-permute-done | bytes 524320 | tf_op jit(solution)/shard_map/ppermute | solution.py:350
  55.9 2.5 %collective-permute-start.5 = (f32[4,64,512]{2,1,0:T(8,128)S(1)}, f32[4,64,512]{2,1,0:T(8,128)S(1)}, u32[]{:S(2)}, u32[]{:S(2)}) collective-permute-start(f32[4,64,512]{2,1,0:T(8,128)S(1)} %pair.5.other), channel_id=1, source_target_pairs={{0,1},{1,0},{2,3},{3,2},{4,5},{5,4},{6,7},{7,6},{8,9},{9,8},{10,11... | collective-permute-start | bytes 1572872 | tf_op jit(solution)/shard_map/ppermute | solution.py:350
  58.4 2.5 %cross.5 = (f32[16,64,512]{2,1,0:T(8,128)S(1)}, f32[4,64,512]{2,1,0:T(8,128)}) custom-call(s32[1]{0:T(128)} %bitcast.7.place, f32[16,64,512]{2,1,0:T(8,128)S(1)} %get-tuple-element.21.now.w1.later, f32[4,64,512]{2,1,0:T(8,128)S(1)} %collective-permute-done.2.halo, f32[16,64,512]{2,1,0:T(8,128)S(1)} %bitcast.27, f32[16,64,512]{2,1,0:T(8,128)S(1)} %copy-done, ...), custom_call_target="tpu_custom_call" | custom-call | flops 10000000 | tf_op jit(solution)/shard_map/cross/pallas_call | solution.py:424
  63.8 1.6 copy-done.4
  68.6 3.0 %inner.6.middle = f32[8,64,512]{2,1,0:T(8,128)S(1)} custom-call(f32[16,64,512]{2,1,0:T(8,128)S(1)} %copy-done.4, f32[16,64,512]{2,1,0:T(8,128)S(1)} %copy-done.8, f32[16,64,512]{2,1,0:T(8,128)S(1)} %copy-done, f32[16,64,512]{2,1,0:T(8,128)S(1)} %copy-done.16), custom_call_target="tpu_custom_call" | custom-call | flops 15000000 | tf_op jit(solution)/shard_map/inner/pallas_call | solution.py:420
  71.8 19.6 %image.1 = (f32[16,64,512]{2,1,0:T(8,128)S(1)}, f32[16,64,512]{2,1,0:T(8,128)S(1)}) custom-call(s32[4]{0:T(128)S(1)} %pad_add_fusion.place, s32[6,16,64,128]{3,2,1,0:T(8,128)S(1)} %bitcast.34, s32[6,16,256]{2,1,0:T(8,128)S(1)} %bitcast.36, f32[1,128]{1,0:T(1,128)S(1)} %pad_bitcast_fusion.table, f32[16,64,512]{2,1,0:T(8,128)S(1)} %bitcast.28, ...), custom_call_target="tpu_custom_call" | custom-call | flops 25000000 | tf_op jit(solution)/shard_map/image/pallas_call | solution.py:440
  91.4 1.6 pair.6.other
  93.0 4.1 %cross.6 = (f32[16,64,512]{2,1,0:T(8,128)}, f32[4,64,512]{2,1,0:T(8,128)S(1)}) custom-call(s32[1]{0:T(128)} %bitcast.7.place, f32[16,64,512]{2,1,0:T(8,128)S(1)} %copy-done.5, f32[4,64,512]{2,1,0:T(8,128)} %collective-permute-done.4.halo, f32[16,64,512]{2,1,0:T(8,128)S(1)} %copy-done.8, f32[16,64,512]{2,1,0:T(8,128)S(1)} %copy-done, ...), custom_call_target="tpu_custom_call" | custom-call | flops 10000000 | tf_op jit(solution)/shard_map/cross/pallas_call | solution.py:424
  97.9 1.6 copy-done.9
  101.9 3.5 %collective-permute-start.9 = (f32[4,64,512]{2,1,0:T(8,128)S(1)}, f32[4,64,512]{2,1,0:T(8,128)S(1)}, u32[]{:S(2)}, u32[]{:S(2)}) collective-permute-start(f32[4,64,512]{2,1,0:T(8,128)S(1)} %pair.6.other), channel_id=1, source_target_pairs={{0,1},{1,0},{2,3},{3,2},{4,5},{5,4},{6,7},{7,6},{8,9},{9,8},{10,11... | collective-permute-start | bytes 1572872 | tf_op jit(solution)/shard_map/ppermute | solution.py:350
  106.9 1.8 %add.50 = f32[2,16,16,512]{3,2,1,0:T(8,128)S(1)} add(f32[2,16,16,512]{3,2,1,0:T(8,128)} %copy-done.20, f32[2,16,16,512]{3,2,1,0:T(8,128)} %collective-permute-done.6) | non-fusion elementwise | flops 262144 | bytes 3145728 | tf_op jit(solution)/shard_map/add | solution.py:468
  111.1 3.5 %collective-permute-start.10 = (f32[8,128]{1,0:T(8,128)S(1)}, f32[8,128]{1,0:T(8,128)S(1)}, u32[]{:S(2)}, u32[]{:S(2)}) collective-permute-start(f32[8,128]{1,0:T(8,128)S(1)} %get-tuple-element.35), channel_id=1, source_target_pairs={{0,1},{1,0},{2,3},{3,2},{4,5},{5,4},{6,7},{7,6},{8,9},{9,8},{10,11... | collective-permute-start | bytes 12296 | tf_op jit(solution)/shard_map/ppermute | solution.py:311
  114.6 14.0 %collective-permute-done.10 = f32[8,128]{1,0:T(8,128)S(1)} collective-permute-done((f32[8,128]{1,0:T(8,128)S(1)}, f32[8,128]{1,0:T(8,128)S(1)}, u32[]{:S(2)}, u32[]{:S(2)}) %collective-permute-start.10) | collective-permute-done | bytes 4128 | tf_op jit(solution)/shard_map/ppermute | solution.py:311
  128.6 2.3 %collective-permute-start.11 = (f32[8,128]{1,0:T(8,128)S(1)}, f32[8,128]{1,0:T(8,128)S(1)}, u32[]{:S(2)}, u32[]{:S(2)}) collective-permute-start(f32[8,128]{1,0:T(8,128)S(1)} %add.55), channel_id=1, source_target_pairs={{0,2},{1,3},{2,0},{3,1},{4,6},{5,7},{6,4},{7,5},{8,10},{9,11},{10,... | collective-permute-start | bytes 12296 | tf_op jit(solution)/shard_map/ppermute | solution.py:311
  132.5 2.2 %collective-permute-start.12 = (f32[8,128]{1,0:T(8,128)S(1)}, f32[8,128]{1,0:T(8,128)S(1)}, u32[]{:S(2)}, u32[]{:S(2)}) collective-permute-start(f32[8,128]{1,0:T(8,128)S(1)} %add.56), channel_id=1, source_target_pairs={{0,4},{1,5},{2,6},{3,7},{4,0},{5,1},{6,2},{7,3},{8,12},{9,13},{10,... | collective-permute-start | bytes 12296 | tf_op jit(solution)/shard_map/ppermute | solution.py:311
  134.7 2.3 %collective-permute-done.12 = f32[8,128]{1,0:T(8,128)S(1)} collective-permute-done((f32[8,128]{1,0:T(8,128)S(1)}, f32[8,128]{1,0:T(8,128)S(1)}, u32[]{:S(2)}, u32[]{:S(2)}) %collective-permute-start.12) | collective-permute-done | bytes 4128 | tf_op jit(solution)/shard_map/ppermute | solution.py:311
  139.7 2.1 %collective-permute-done.14 = f32[8,128]{1,0:T(8,128)S(1)} collective-permute-done((f32[8,128]{1,0:T(8,128)S(1)}, f32[8,128]{1,0:T(8,128)S(1)}, u32[]{:S(2)}, u32[]{:S(2)}) %collective-permute-start.14) | collective-permute-done | bytes 4128 | tf_op jit(solution)/shard_map/ppermute | solution.py:311
  147.7 3.0 %inner.7.middle = f32[8,64,512]{2,1,0:T(8,128)S(1)} custom-call(f32[16,64,512]{2,1,0:T(8,128)S(1)} %copy-done.10, f32[16,64,512]{2,1,0:T(8,128)S(1)} %copy-done.6, f32[16,64,512]{2,1,0:T(8,128)S(1)} %copy-done, f32[16,64,512]{2,1,0:T(8,128)S(1)} %copy-done.14), custom_call_target="tpu_custom_call" | custom-call | flops 15000000 | tf_op jit(solution)/shard_map/inner/pallas_call | solution.py:420
  150.7 1.6 pair.7.other
  152.3 4.4 %cross.7 = (f32[16,64,512]{2,1,0:T(8,128)}, f32[4,64,512]{2,1,0:T(8,128)}) custom-call(s32[1]{0:T(128)} %bitcast.7.place, f32[16,64,512]{2,1,0:T(8,128)S(1)} %copy-done.11, f32[4,64,512]{2,1,0:T(8,128)} %collective-permute-done.8.halo, f32[16,64,512]{2,1,0:T(8,128)S(1)} %copy-done.6, f32[16,64,512]{2,1,0:T(8,128)S(1)} %copy-done, ...), custom_call_target="tpu_custom_call" | custom-call | flops 10000000 | tf_op jit(solution)/shard_map/cross/pallas_call | solution.py:424
  156.7 1.9 %add_bitcast_fusion = f32[16,16,512]{2,1,0:T(8,128)} fusion(f32[1,16,16,512]{3,2,1,0:T(8,128)} %collective-permute-done.7, f32[2,16,16,512]{3,2,1,0:T(8,128)S(1)} %copy-done.26, s32[]{:T(128)S(6)} %select_n.40), kind=kLoop, calls=%fused_computation | loop fusion | flops 131072 | bytes 1572868 | tf_op jit(solution)/shard_map/squeeze | solution.py:476
  (83 shorter events, 27.5 us)
Async XLA Ops:
  0.6 6.0 %copy-start.27 = (f32[64]{0:T(128)S(1)}, f32[64]{0:T(128)}, u32[]{:S(2)}) copy-start(f32[64]{0:T(128)} %param.14) | copy-start | bytes 772
  0.6 6.0 %copy-start.21 = (s32[1,6,16,256]{3,2,1,0:T(8,128)S(1)}, s32[1,6,16,256]{3,2,1,0:T(8,128)}, u32[]{:S(2)}) copy-start(s32[1,6,16,256]{3,2,1,0:T(8,128)} %param.13) | copy-start | bytes 294916
  0.7 6.0 %copy-start.22 = (f32[1,4,256]{2,1,0:T(4,128)S(1)}, f32[1,4,256]{2,1,0:T(4,128)}, u32[]{:S(2)}) copy-start(f32[1,4,256]{2,1,0:T(4,128)} %param.16) | copy-start | bytes 12292
  0.7 6.0 %copy-start.23 = (s32[1,256]{1,0:T(1,128)S(1)}, s32[1,256]{1,0:T(1,128)}, u32[]{:S(2)}) copy-start(s32[1,256]{1,0:T(1,128)} %cell.1) | copy-start | bytes 3076
  3.0 14.5 %copy-start = (f32[16,64,512]{2,1,0:T(8,128)S(1)}, f32[16,64,512]{2,1,0:T(8,128)}, u32[]{:S(2)}) copy-start(f32[16,64,512]{2,1,0:T(8,128)} %courant.23) | copy-start | bytes 6291460
  3.0 25.7 %collective-permute-start.1 = (f32[4,64,512]{2,1,0:T(8,128)}, f32[4,64,512]{2,1,0:T(8,128)S(1)}, u32[]{:S(2)}, u32[]{:S(2)}) collective-permute-start(f32[4,64,512]{2,1,0:T(8,128)} %get-tuple-element.36), channel_id=1, source_target_pairs={{0,1},{1,0},{2,3},{3,2},{4,5},{5,4},{6,7},{7,6},{8,9},{9,8},{10,11... | collective-permute-start | bytes 1572872 | tf_op jit(solution)/shard_map/ppermute | solution.py:350
  5.9 26.8 %collective-permute-start = (f32[4,64,512]{2,1,0:T(8,128)}, f32[4,64,512]{2,1,0:T(8,128)S(1)}, u32[]{:S(2)}, u32[]{:S(2)}) collective-permute-start(f32[4,64,512]{2,1,0:T(8,128)} %get-tuple-element.37), channel_id=1, source_target_pairs={{1,2},{3,4},{5,6},{2,1},{4,3},{6,5},{9,10},{11,12},{13,14},{10,9},... | collective-permute-start | bytes 1572872 | tf_op jit(solution)/shard_map/ppermute | solution.py:353
  17.4 7.7 %copy-start.13 = (f32[16,64,512]{2,1,0:T(8,128)}, f32[16,64,512]{2,1,0:T(8,128)S(1)}, u32[]{:S(2)}) copy-start(f32[16,64,512]{2,1,0:T(8,128)S(1)} %get-tuple-element.33.added) | copy-start | bytes 6291460
  17.4 7.7 %copy-start.15 = (f32[16,64,512]{2,1,0:T(8,128)}, f32[16,64,512]{2,1,0:T(8,128)S(1)}, u32[]{:S(2)}) copy-start(f32[16,64,512]{2,1,0:T(8,128)S(1)} %get-tuple-element.28.added) | copy-start | bytes 6291460
  17.5 3.1 %copy-start.1 = (f32[1,16,64,512]{3,2,1,0:T(8,128)S(1)}, f32[1,16,64,512]{3,2,1,0:T(8,128)}, u32[]{:S(2)}) copy-start(f32[1,16,64,512]{3,2,1,0:T(8,128)} %param.9) | copy-start | bytes 6291460
  30.3 24.0 %collective-permute-start.3 = (f32[4,64,512]{2,1,0:T(8,128)S(1)}, f32[4,64,512]{2,1,0:T(8,128)S(1)}, u32[]{:S(2)}, u32[]{:S(2)}) collective-permute-start(f32[4,64,512]{2,1,0:T(8,128)S(1)} %pair.4.other), channel_id=1, source_target_pairs={{0,1},{1,0},{2,3},{3,2},{4,5},{5,4},{6,7},{7,6},{8,9},{9,8},{10,11... | collective-permute-start | bytes 1572872 | tf_op jit(solution)/shard_map/ppermute | solution.py:350
  34.5 24.0 %copy-start.7 = (f32[16,64,512]{2,1,0:T(8,128)}, f32[16,64,512]{2,1,0:T(8,128)S(1)}, u32[]{:S(2)}) copy-start(f32[16,64,512]{2,1,0:T(8,128)S(1)} %get-tuple-element.21.now.w1.later) | copy-start | bytes 6291460
  34.5 23.9 %collective-permute-start.2 = (f32[4,64,512]{2,1,0:T(8,128)S(1)}, f32[4,64,512]{2,1,0:T(8,128)S(1)}, u32[]{:S(2)}, u32[]{:S(2)}) collective-permute-start(f32[4,64,512]{2,1,0:T(8,128)S(1)} %get-tuple-element.22), channel_id=1, source_target_pairs={{1,2},{3,4},{5,6},{2,1},{4,3},{6,5},{9,10},{11,12},{13,14},{10,9},... | collective-permute-start | bytes 1572872 | tf_op jit(solution)/shard_map/ppermute | solution.py:353
  55.9 7.9 %copy-start.28 = (s32[1,3]{1,0:T(1,128)S(1)}, s32[1,3]{1,0:T(1,128)}, u32[]{:S(2)}) copy-start(s32[1,3]{1,0:T(1,128)} %param.17) | copy-start | bytes 40
  55.9 35.5 %collective-permute-start.5 = (f32[4,64,512]{2,1,0:T(8,128)S(1)}, f32[4,64,512]{2,1,0:T(8,128)S(1)}, u32[]{:S(2)}, u32[]{:S(2)}) collective-permute-start(f32[4,64,512]{2,1,0:T(8,128)S(1)} %pair.5.other), channel_id=1, source_target_pairs={{0,1},{1,0},{2,3},{3,2},{4,5},{5,4},{6,7},{7,6},{8,9},{9,8},{10,11... | collective-permute-start | bytes 1572872 | tf_op jit(solution)/shard_map/ppermute | solution.py:350
  62.3 30.7 %collective-permute-start.4 = (f32[4,64,512]{2,1,0:T(8,128)}, f32[4,64,512]{2,1,0:T(8,128)}, u32[]{:S(2)}, u32[]{:S(2)}) collective-permute-start(f32[4,64,512]{2,1,0:T(8,128)} %get-tuple-element.27), channel_id=1, source_target_pairs={{1,2},{3,4},{5,6},{2,1},{4,3},{6,5},{9,10},{11,12},{13,14},{10,9},... | collective-permute-start | bytes 1572872 | tf_op jit(solution)/shard_map/ppermute | solution.py:353
  68.6 3.0 %copy-start.2 = (f32[1,16,64,512]{3,2,1,0:T(8,128)S(1)}, f32[1,16,64,512]{3,2,1,0:T(8,128)}, u32[]{:S(2)}) copy-start(f32[1,16,64,512]{3,2,1,0:T(8,128)} %param.9) | copy-start | bytes 6291460
  68.6 3.0 %copy-start.5 = (f32[16,64,512]{2,1,0:T(8,128)S(1)}, f32[16,64,512]{2,1,0:T(8,128)}, u32[]{:S(2)}) copy-start(f32[16,64,512]{2,1,0:T(8,128)} %copy-done.3) | copy-start | bytes 6291460
  68.6 3.2 %copy-start.19 = (s32[1,6,16,64,128]{4,3,2,1,0:T(8,128)S(1)}, s32[1,6,16,64,128]{4,3,2,1,0:T(8,128)}, u32[]{:S(2)}) copy-start(s32[1,6,16,64,128]{4,3,2,1,0:T(8,128)} %param.12) | copy-start | bytes 9437188
  71.8 19.6 %copy-start.17 = (f32[16,64,512]{2,1,0:T(8,128)S(1)}, f32[16,64,512]{2,1,0:T(8,128)}, u32[]{:S(2)}) copy-start(f32[16,64,512]{2,1,0:T(8,128)} %copy-done.15) | copy-start | bytes 6291460
  101.9 5.0 %collective-permute-start.6 = (f32[2,16,16,512]{3,2,1,0:T(8,128)}, f32[2,16,16,512]{3,2,1,0:T(8,128)}, u32[]{:S(2)}, u32[]{:S(2)}) collective-permute-start(f32[2,16,16,512]{3,2,1,0:T(8,128)} %get-tuple-element.31), channel_id=1, source_target_pairs={{0,8},{8,0},{16,24},{24,16},{1,9},{9,1},{17,25},{25,17},{2,10},{10... | collective-permute-start | bytes 3145736 | tf_op jit(solution)/shard_map/ppermute | solution.py:468
  101.9 48.8 %collective-permute-start.9 = (f32[4,64,512]{2,1,0:T(8,128)S(1)}, f32[4,64,512]{2,1,0:T(8,128)S(1)}, u32[]{:S(2)}, u32[]{:S(2)}) collective-permute-start(f32[4,64,512]{2,1,0:T(8,128)S(1)} %pair.6.other), channel_id=1, source_target_pairs={{0,1},{1,0},{2,3},{3,2},{4,5},{5,4},{6,7},{7,6},{8,9},{9,8},{10,11... | collective-permute-start | bytes 1572872 | tf_op jit(solution)/shard_map/ppermute | solution.py:350
  105.4 46.9 %collective-permute-start.8 = (f32[4,64,512]{2,1,0:T(8,128)}, f32[4,64,512]{2,1,0:T(8,128)}, u32[]{:S(2)}, u32[]{:S(2)}) collective-permute-start(f32[4,64,512]{2,1,0:T(8,128)} %copy-done.24), channel_id=1, source_target_pairs={{1,2},{3,4},{5,6},{2,1},{4,3},{6,5},{9,10},{11,12},{13,14},{10,9},... | collective-permute-start | bytes 1572872 | tf_op jit(solution)/shard_map/ppermute | solution.py:353
  108.6 20.0 %copy-start.25 = (f32[2,16,16,512]{3,2,1,0:T(8,128)}, f32[2,16,16,512]{3,2,1,0:T(8,128)S(1)}, u32[]{:S(2)}) copy-start(f32[2,16,16,512]{3,2,1,0:T(8,128)S(1)} %add.50) | copy-start | bytes 3145732
  109.5 47.2 %collective-permute-start.7 = (f32[1,16,16,512]{3,2,1,0:T(8,128)}, f32[1,16,16,512]{3,2,1,0:T(8,128)}, u32[]{:S(2)}, u32[]{:S(2)}) collective-permute-start(f32[1,16,16,512]{3,2,1,0:T(8,128)} %constant_dynamic-slice_fusion), channel_id=1, source_target_pairs={{0,16},{8,24},{16,0},{24,8},{1,17},{9,25},{17,1},{25,9},{2,18},{10... | collective-permute-start | bytes 1572872 | tf_op jit(solution)/shard_map/ppermute | solution.py:468
  111.1 17.5 %collective-permute-start.10 = (f32[8,128]{1,0:T(8,128)S(1)}, f32[8,128]{1,0:T(8,128)S(1)}, u32[]{:S(2)}, u32[]{:S(2)}) collective-permute-start(f32[8,128]{1,0:T(8,128)S(1)} %get-tuple-element.35), channel_id=1, source_target_pairs={{0,1},{1,0},{2,3},{3,2},{4,5},{5,4},{6,7},{7,6},{8,9},{9,8},{10,11... | collective-permute-start | bytes 12296 | tf_op jit(solution)/shard_map/ppermute | solution.py:311
  128.6 3.9 %collective-permute-start.11 = (f32[8,128]{1,0:T(8,128)S(1)}, f32[8,128]{1,0:T(8,128)S(1)}, u32[]{:S(2)}, u32[]{:S(2)}) collective-permute-start(f32[8,128]{1,0:T(8,128)S(1)} %add.55), channel_id=1, source_target_pairs={{0,2},{1,3},{2,0},{3,1},{4,6},{5,7},{6,4},{7,5},{8,10},{9,11},{10,... | collective-permute-start | bytes 12296 | tf_op jit(solution)/shard_map/ppermute | solution.py:311
  132.5 4.5 %collective-permute-start.12 = (f32[8,128]{1,0:T(8,128)S(1)}, f32[8,128]{1,0:T(8,128)S(1)}, u32[]{:S(2)}, u32[]{:S(2)}) collective-permute-start(f32[8,128]{1,0:T(8,128)S(1)} %add.56), channel_id=1, source_target_pairs={{0,4},{1,5},{2,6},{3,7},{4,0},{5,1},{6,2},{7,3},{8,12},{9,13},{10,... | collective-permute-start | bytes 12296 | tf_op jit(solution)/shard_map/ppermute | solution.py:311
  137.0 1.2 collective-permute-start.13
  138.2 3.6 %collective-permute-start.14 = (f32[8,128]{1,0:T(8,128)S(1)}, f32[8,128]{1,0:T(8,128)S(1)}, u32[]{:S(2)}, u32[]{:S(2)}) collective-permute-start(f32[8,128]{1,0:T(8,128)S(1)} %add.58), channel_id=1, source_target_pairs={{0,16},{8,24},{16,0},{24,8},{1,17},{9,25},{17,1},{25,9},{2,18},{10... | collective-permute-start | bytes 12296 | tf_op jit(solution)/shard_map/ppermute | solution.py:311
  147.7 3.0 %copy-start.11 = (f32[16,64,512]{2,1,0:T(8,128)S(1)}, f32[16,64,512]{2,1,0:T(8,128)}, u32[]{:S(2)}) copy-start(f32[16,64,512]{2,1,0:T(8,128)} %get-tuple-element.29.w3.now) | copy-start | bytes 6291460
  152.3 4.4 %copy-start.26 = (f32[2,16,16,512]{3,2,1,0:T(8,128)S(1)}, f32[2,16,16,512]{3,2,1,0:T(8,128)}, u32[]{:S(2)}) copy-start(f32[2,16,16,512]{3,2,1,0:T(8,128)} %copy-done.25) | copy-start | bytes 3145732
  (12 other events, 17.8 us)

commit v2 on v1

--- a/solution.py
+++ b/solution.py
@@ -6,6 +6,7 @@
 from jax.experimental import pallas as pl
 from jax.experimental.pallas import tpu as pltpu
 from jax.sharding import PartitionSpec as P
+
 
 ITERS = 4
 MUTE = 8
@@ -95,7 +96,7 @@
 
 
 def edge(place, now, halo, later, courant, added, strip, ypad, column):
-    depth, rows, cols = now.shape
+    depth, _, _ = now.shape
     first = place[0]
     high = first > 0
     halo_at = jnp.where(high, 2 * REACH, 0)
@@ -196,7 +197,9 @@
             preferred_element_type=jnp.float32,
         )
         entry = jnp.sum(jnp.where(at_block, entries, 0.0), axis=1, keepdims=True)
-        at_entry = lax.broadcasted_iota(jnp.int32, (count, LANES), 1) == entry.astype(jnp.int32)
+        at_entry = lax.broadcasted_iota(jnp.int32, (count, table.shape[1]), 1) == entry.astype(
+            jnp.int32
+        )
         scale = jnp.sum(jnp.where(at_entry, table[...], 0.0), axis=1, keepdims=True)
         residual = picked * scale - turned[:, SUB + level - 1 : SUB + level]
         total = total + residual * residual
@@ -226,12 +229,13 @@
 
 
 def image_kernel(
-    place, codes, index, table, w0, w1, w2, image, last, packed, turned, ey
+    first, source, codes, index, table, w0, w1, w2, image, last, packed, turned, ey, held, field
 ):
-    levels, depth, rows, words = codes.shape
+    levels, depth, rows, _ = codes.shape
     cols = image.shape[2]
     tiles = cols // LANES
-    first_z, source_z, source_y, source_x = (place[k] for k in range(4))
+    first_z = first[0]
+    source_z, source_y, source_x = (source[0, k] for k in range(3))
     scale_by = -1.0 / (2.0 * MUTE * MUTE)
     lane = lax.broadcasted_iota(jnp.int32, (SUB, LANES), 1)
 
@@ -242,7 +246,8 @@
     packed[...] = jnp.zeros(packed.shape, jnp.float32)
     lines = levels * depth
     chosen = index[...].reshape(lines, rows * tiles)
-    across = jnp.broadcast_to(table[...], (lines, LANES))
+    held[0:1, 0 : table.shape[1]] = table[...]
+    across = jnp.broadcast_to(held[0:1, :], (lines, LANES))
     for h in range(rows * tiles // LANES):
         cut = slice(h * LANES, (h + 1) * LANES)
         packed[0:lines, cut] = jnp.take_along_axis(
@@ -253,43 +258,58 @@
     ex = [bell(lane + (t * LANES) - source_x) for t in range(tiles)]
 
     def plane(z, carry):
+        turn = lax.rem(LANES - z, LANES)
+        for t in range(tiles):
+            for r in range(rows // SUB):
+                held[t * rows + r * SUB : t * rows + (r + 1) * SUB, :] = pltpu.roll(
+                    turned[pl.ds(t + tiles * SUB * r, SUB, stride=tiles), :], turn, 1
+                )
+        for level in range(levels):
+            lane_at = slice(level * depth, level * depth + 1)
+            for r in range(rows // SUB):
+                y = slice(r * SUB, (r + 1) * SUB)
+                word = codes[level, z, y, :]
+                for t in range(tiles):
+                    at = slice(t * rows + r * SUB, t * rows + (r + 1) * SUB)
+                    scale = jnp.broadcast_to(held[at, lane_at], (SUB, LANES))
+                    code = jnp.bitwise_and(jnp.right_shift(word, 8 * t), 255) - 128
+                    field[level, y, t * LANES : (t + 1) * LANES] = code.astype(jnp.float32) * scale
         ez = bell(jnp.full((SUB, LANES), first_z + z - source_z, jnp.int32))
         for r in range(rows // SUB):
             y = slice(r * SUB, (r + 1) * SUB)
-            word = [codes[level, z, y, :] for level in range(levels)]
             down = ez * ey[y, :]
             for t in range(tiles):
                 x = slice(t * LANES, (t + 1) * LANES)
-                scales = pltpu.roll(
-                    turned[pl.ds(t + tiles * SUB * r, SUB, stride=tiles), :],
-                    lax.rem(LANES - z, LANES),
-                    1,
-                )
-                field = []
-                for level in range(levels):
-                    code = jnp.bitwise_and(jnp.right_shift(word[level], 8 * t), 255) - 128
-                    scale = jnp.broadcast_to(
-                        scales[:, level * depth : level * depth + 1], (SUB, LANES)
-                    )
-                    field.append(code.astype(jnp.float32) * scale)
+                value = [field[level, y, x] for level in range(levels)]
                 bend = [
                     None if k in (0, levels - 1)
-                    else (field[k + 1] - 2.0 * field[k]) + field[k - 1]
+                    else (value[k + 1] - 2.0 * value[k]) + value[k - 1]
                     for k in range(levels)
                 ]
                 mute = 1.0 - down * ex[t]
-                value = w0[z, y, x] * bend[ITERS]
-                value = value + w1[z, y, x] * bend[ITERS - 1]
-                value = value + w2[z, y, x] * bend[ITERS - 2]
-                image[z, y, x] = mute * value
+                terms = w0[z, y, x] * bend[ITERS]
+                terms = terms + w1[z, y, x] * bend[ITERS - 1]
+                terms = terms + w2[z, y, x] * bend[ITERS - 2]
+                image[z, y, x] = mute * terms
                 last[z, y, x] = mute * bend[ITERS - 3]
         return carry
 
     lax.fori_loop(0, depth, plane, 0)
 
 
+def cut_kernel(place, now, after, strip):
+    del after
+    first = place[0]
+
+    def step(j, carry):
+        strip[j] = now[first + j]
+        return carry
+
+    lax.fori_loop(0, REACH, step, 0)
+
+
 def split_kernel(side, image, last, w3, kept, sent):
-    half, depth, block, cols = kept.shape
+    half, depth, block, _ = kept.shape
     mine = side[0]
 
     def plane(z, carry):
@@ -302,15 +322,59 @@
     lax.fori_loop(0, depth, plane, 0)
 
 
-def summed(value, axis):
-    count = lax.axis_size(axis)
-    if count & (count - 1):
-        return lax.psum(value, axis)
-    hop = 1
-    while hop < count:
-        value = value + lax.ppermute(value, axis, [(i, i ^ hop) for i in range(count)])
-        hop *= 2
-    return value
+def halve_kernel(side, kept, arrived, keep, send):
+    half, depth, _, _ = keep.shape
+    mine = side[0]
+
+    def plane(z, carry):
+        for q in range(half):
+            for out, which in ((keep, mine), (send, 1 - mine)):
+                out[q, z] = kept[2 * q + which, z] + arrived[2 * q + which, z]
+        return carry
+
+    lax.fori_loop(0, depth, plane, 0)
+
+
+def add_kernel(one, other, out):
+    def plane(z, carry):
+        out[z] = one[z] + other[z]
+        return carry
+
+    lax.fori_loop(0, out.shape[0], plane, 0)
+
+
+def tile_add_kernel(one, other, out):
+    out[...] = one[...] + other[...]
+
+
+def scalar_kernel(factor, one, other, out):
+    out[0, 0] = ((one[...] + other[...]) * factor)[0, 0]
+
+
+def misfit_of(squares, factor):
+    hops = []
+    for axis, name in (("space", "m"), ("shot", "n")):
+        count = lax.axis_size(axis)
+        if count & (count - 1):
+            squares = lax.psum(squares, axis)
+            continue
+        hop = 1
+        while hop < count:
+            hops.append((axis, f"{name}{hop}", [(i, i ^ hop) for i in range(count)]))
+            hop *= 2
+    for k, (axis, name, moves) in enumerate(hops):
+        arrived = lax.ppermute(squares, axis, moves)
+        last = k + 1 == len(hops)
+        squares = pl.pallas_call(
+            functools.partial(scalar_kernel, factor) if last else tile_add_kernel,
+            out_shape=jax.ShapeDtypeStruct((1, 1) if last else squares.shape, jnp.float32),
+            in_specs=[VMEM] * 2,
+            out_specs=SMEM if last else VMEM,
+            compiler_params=params(4),
+            cost_estimate=cost(0.2),
+            name="tally",
+        )(squares, arrived)
+    return squares
 
 
 def body(
@@ -364,7 +428,7 @@
         in_specs=[VMEM] * 4,
         out_specs=VMEM,
         scratch_shapes=[pltpu.VMEM((depth - 2 * REACH,) + ypad, jnp.float32)],
-        compiler_params=params(20),
+        compiler_params=params(10),
         cost_estimate=cost(3),
         name="inner",
     )
@@ -374,7 +438,7 @@
         in_specs=[SMEM] + [VMEM] * 5,
         out_specs=VMEM,
         scratch_shapes=edge_scratch,
-        compiler_params=params(20),
+        compiler_params=params(10),
         cost_estimate=cost(2),
         name="pair",
     )
@@ -384,16 +448,15 @@
         in_specs=[SMEM] + [VMEM] * 7,
         out_specs=(VMEM, VMEM),
         scratch_shapes=edge_scratch,
-        compiler_params=params(20),
+        compiler_params=params(10),
         cost_estimate=cost(2),
         name="cross",
     )
 
     pair_halo = pair_exchange(lax.dynamic_slice_in_dim(now, pair_place, REACH, 0))
-    cross_halo = cross_exchange(lax.dynamic_slice_in_dim(now, cross_place, REACH, 0))
-
-    table = jnp.pad(scale_table, (0, LANES - scale_table.shape[0])).reshape(1, LANES)
-    *added, squares = pl.pallas_call(
+
+    table = scale_table.reshape(1, scale_table.shape[0])
+    sources = pl.pallas_call(
         source_kernel,
         out_shape=[field] * ITERS + [jax.ShapeDtypeStruct((SUB, LANES), jnp.float32)],
         in_specs=[SMEM] + [VMEM] * 5,
@@ -402,10 +465,11 @@
             pltpu.VMEM((LANES, receivers), jnp.float32),
             pltpu.VMEM((receivers, depth * rows), jnp.bfloat16),
         ],
-        compiler_params=params(28),
+        compiler_params=params(14),
         cost_estimate=cost(8),
         name="sources",
-    )(
+    )
+    *added, squares = sources(
         (first_z * (rows * cols)).reshape(1).astype(jnp.int32),
         receiver_cell,
         codes,
@@ -413,6 +477,17 @@
         table,
         observed[0],
     )
+
+    cross_sent = pl.pallas_call(
+        cut_kernel,
+        out_shape=strip,
+        in_specs=[SMEM, VMEM, ANY],
+        out_specs=VMEM,
+        compiler_params=params(6),
+        cost_estimate=cost(1),
+        name="cut",
+    )(cross_place.reshape(1), now, squares)
+    cross_halo = cross_exchange(cross_sent)
 
     waves = [now]
     for step in range(ITERS):
@@ -436,47 +511,72 @@
         later = now
         waves.append(new)
 
-    place = jnp.concatenate([first_z.reshape(1).astype(jnp.int32), source_cell[0]])
-    image, last = pl.pallas_call(
+    images = pl.pallas_call(
         image_kernel,
         out_shape=(field, field),
-        in_specs=[SMEM] + [VMEM] * 6,
+        in_specs=[SMEM] * 2 + [VMEM] * 6,
         out_specs=(VMEM, VMEM),
         scratch_shapes=[
             pltpu.VMEM((LANES, rows * tiles), jnp.float32),
             pltpu.VMEM((rows * tiles, LANES), jnp.float32),
             pltpu.VMEM((rows, LANES), jnp.float32),
+            pltpu.VMEM((tiles * rows, LANES), jnp.float32),
+            pltpu.VMEM((levels, rows, cols), jnp.float32),
         ],
-        compiler_params=params(28),
+        compiler_params=params(12),
         cost_estimate=cost(5),
         name="image",
-    )(place, codes, index, table, waves[0], waves[1], waves[2])
+    )
+    image, last = images(
+        first_z.reshape(1).astype(jnp.int32),
+        source_cell,
+        codes,
+        index,
+        table,
+        waves[0],
+        waves[1],
+        waves[2],
+    )
 
     block = rows // shots
     part = jax.ShapeDtypeStruct((shots // 2, depth, block, cols), jnp.float32)
-    kept, sent = pl.pallas_call(
+    splits = pl.pallas_call(
         split_kernel,
         out_shape=(part, part),
         in_specs=[SMEM] + [VMEM] * 3,
         out_specs=(VMEM, VMEM),
-        compiler_params=params(20),
+        compiler_params=params(10),
         cost_estimate=cost(2),
         name="split",
-    )((shot % 2).reshape(1).astype(jnp.int32), image, last, waves[3])
+    )
+    kept, sent = splits((shot % 2).reshape(1).astype(jnp.int32), image, last, waves[3])
     hop = 1
     while True:
-        kept = kept + lax.ppermute(sent, "shot", [(i, i ^ hop) for i in range(shots)])
+        arrived = lax.ppermute(sent, "shot", [(i, i ^ hop) for i in range(shots)])
         hop *= 2
         if hop >= shots:
             break
-        mine = (shot // hop) % 2
-        halves = kept.reshape((kept.shape[0] // 2, 2) + kept.shape[1:])
-        kept = lax.dynamic_index_in_dim(halves, mine, 1, keepdims=False)
-        sent = lax.dynamic_index_in_dim(halves, 1 - mine, 1, keepdims=False)
-    gradient = kept[0]
-
-    squares = summed(summed(squares, "space"), "shot")
-    misfit = 0.5 * squares[0, 0] / (shots * ITERS * receivers * slabs)
+        part = jax.ShapeDtypeStruct((kept.shape[0] // 2,) + kept.shape[1:], jnp.float32)
+        kept, sent = pl.pallas_call(
+            halve_kernel,
+            out_shape=(part, part),
+            in_specs=[SMEM] + [VMEM] * 2,
+            out_specs=(VMEM, VMEM),
+            compiler_params=params(8),
+            cost_estimate=cost(1),
+            name="halve",
+        )(((shot // hop) % 2).reshape(1).astype(jnp.int32), kept, arrived)
+    gradient = pl.pallas_call(
+        add_kernel,
+        out_shape=jax.ShapeDtypeStruct(kept.shape[1:], jnp.float32),
+        in_specs=[VMEM] * 2,
+        out_specs=VMEM,
+        compiler_params=params(8),
+        cost_estimate=cost(1),
+        name="finish",
+    )(kept[0], arrived[0])
+
+    misfit = misfit_of(squares, 0.5 / (shots * ITERS * receivers * slabs)).reshape(())
     return (gradient, waves[4][None], waves[3][None], misfit)
 
 

time: 161 us -> 154 us (0.957)
  Pallas kernels: 60.8 us -> 51.4 us
  local copies, waits for them, and re-layouts: 24.8 us -> 32.6 us
  starting transfers between devices: 26.8 us -> 31.2 us
  waiting for transfers between devices: 40.9 us -> 37 us
  other arithmetic: 3.8 us -> 0 us
  between operations: 2.81 us -> 1.01 us
    unnamed x58 -> x76, local copies, waits for them, and re-layouts: 21.1 us -> 31.5 us
    pallas_call x3 -> x11, Pallas kernels: 29.8 us -> 20.5 us  [the longest x1 8.82 us: body(): sources((first_z * (rows * cols)).reshape(1).astype(jnp.int32), receiver_...]
    ppermute x4, waiting for transfers between devices: 19.7 us -> 16.7 us  [pair_exchange(): return lax.ppermute(block, 'space', pairs)]
    ppermute x7, starting transfers between devices: 11 us -> 13.3 us  [the longest x5 11.7 us: misfit_of(): arrived = lax.ppermute(squares, axis, moves)]
    ppermute x4, starting transfers between devices: 11.5 us -> 13.5 us  [pair_exchange(): return lax.ppermute(block, 'space', pairs)]
    squeeze x1 -> x0, other arithmetic: 1.95 us -> none  [body(): gradient = kept[0]]
    add x6 -> x0, other arithmetic: 1.77 us -> none  [the longest x1 1.76 us: body(): kept + lax.ppermute(sent, 'shot', [(i, i ^ hop) for i in range(shots)])]
  transfers between devices with their start and end apart: 15 -> 15, of which waited for: 7 -> 6; matrix products, arithmetic and copies ran while one was open for 2% -> 0% of each run, Pallas kernels for 35% -> 29%
where the time goes in v2:
time: 154 us; the launch traced here: 153 us
  Pallas kernels  51.4 us (33%)
  waiting for transfers between devices  37 us (24%)
  local copies, waits for them, and re-layouts  32.6 us (21%)
  starting transfers between devices  31.2 us (20%)
    unnamed x76, local copies, waits for them, and re-layouts  31.5 us
    ppermute x5, waiting for transfers between devices, misfit_of(): arrived = lax.ppermute(squares, axis, moves)  20.3 us
    ppermute x4, waiting for transfers between devices, pair_exchange(): return lax.ppermute(block, 'space', pairs)  16.7 us
    ppermute x4, starting transfers between devices, pair_exchange(): return lax.ppermute(block, 'space', pairs)  13.5 us
    pallas_call x4, Pallas kernels, body(): cross(cross_place.reshape(1), now, cross_halo, later, courant, added[step...  12.7 us
    pallas_call x4, Pallas kernels, body(): within = inner(now, later, courant, added[step])  11.8 us
    ppermute x5, starting transfers between devices, misfit_of(): arrived = lax.ppermute(squares, axis, moves)  11.7 us
    pallas_call x1, Pallas kernels, body(): sources((first_z * (rows * cols)).reshape(1).astype(jnp.int32), receiver_...  8.82 us
  transfers between devices with their start and end apart: 15, of which 6 were waited for; matrix products, arithmetic and copies ran while one was open for 0% of the time, Pallas kernels for 29%

profile of v2, /device:TPU:0, one launch (start us, length us, event | category | flops | bytes accessed | tf_op | source)
XLA Modules:
  0.0 153.2 jit_solution(3900971022768626785)
XLA Ops:
  1.7 3.0 %collective-permute-start.1 = (f32[4,64,512]{2,1,0:T(8,128)S(1)}, f32[4,64,512]{2,1,0:T(8,128)S(1)}, u32[]{:S(2)}, u32[]{:S(2)}) collective-permute-start(f32[4,64,512]{2,1,0:T(8,128)S(1)} %dynamic-slice_bitcast_fusion), channel_id=1, source_target_pairs={{0,1},{1,0},{2,3},{3,2},{4,5},{5,4},{6,7},{7,6},{8,9},{9,8},{10,11... | collective-permute-start | bytes 1572872 | tf_op jit(solution)/shard_map/ppermute | solution.py:414
  4.8 1.9 %copy-done.26 = s32[1,6,16,64,128]{4,3,2,1,0:T(8,128)S(1)} copy-done((s32[1,6,16,64,128]{4,3,2,1,0:T(8,128)S(1)}, s32[1,6,16,64,128]{4,3,2,1,0:T(8,128)}, u32[]{:S(2)}) %copy-start.26) | copy-done | bytes 3145752
  9.6 8.8 %sources.1 = (f32[16,64,512]{2,1,0:T(8,128)S(1)}, f32[16,64,512]{2,1,0:T(8,128)S(1)}, f32[16,64,512]{2,1,0:T(8,128)S(1)}, f32[16,64,512]{2,1,0:T(8,128)S(1)}, f32[8,128]{1,0:T(8,128)S(1)}) custom-call(s32[1]{0:T(128)} %bitcast.8.first, s32[1,256]{1,0:T(1,128)S(1)} %copy-done.35, s32[6,16,64,128]{3,2,1,0:T(8,128)S(1)} %bitcast.31, ...), custom_call_target="tpu_custom_call" | custom-call | flops 40000000 | tf_op jit(solution)/shard_map/sources/pallas_call | solution.py:472
  23.7 1.7 %copy-done.1 = f32[1,16,64,512]{3,2,1,0:T(8,128)S(1)} copy-done((f32[1,16,64,512]{3,2,1,0:T(8,128)S(1)}, f32[1,16,64,512]{3,2,1,0:T(8,128)}, u32[]{:S(2)}) %copy-start.1) | copy-done | bytes 2097176
  27.8 1.6 %copy-done.15 = f32[1,16,64,512]{3,2,1,0:T(8,128)S(1)} copy-done((f32[1,16,64,512]{3,2,1,0:T(8,128)S(1)}, f32[1,16,64,512]{3,2,1,0:T(8,128)}, u32[]{:S(2)}) %copy-start.15) | copy-done | bytes 2097176
  29.4 1.6 %copy-done.25 = f32[16,64,512]{2,1,0:T(8,128)S(1)} copy-done((f32[16,64,512]{2,1,0:T(8,128)S(1)}, f32[16,64,512]{2,1,0:T(8,128)}, u32[]{:S(2)}) %copy-start.25) | copy-done | bytes 2097176
  31.0 3.0 %inner.4.middle = f32[8,64,512]{2,1,0:T(8,128)S(1)} custom-call(f32[16,64,512]{2,1,0:T(8,128)S(1)} %bitcast.20, f32[16,64,512]{2,1,0:T(8,128)S(1)} %bitcast.28, f32[16,64,512]{2,1,0:T(8,128)S(1)} %copy-done, f32[16,64,512]{2,1,0:T(8,128)S(1)} %copy-done.25), custom_call_target="tpu_custom_call" | custom-call | flops 15000000 | tf_op jit(solution)/shard_map/inner/pallas_call | solution.py:495
  34.0 1.6 %pair.4.other = f32[4,64,512]{2,1,0:T(8,128)S(1)} custom-call(s32[1]{0:T(128)} %bitcast.11.place, f32[16,64,512]{2,1,0:T(8,128)S(1)} %bitcast.21, f32[4,64,512]{2,1,0:T(8,128)S(1)} %collective-permute-done.1.halo, f32[16,64,512]{2,1,0:T(8,128)S(1)} %bitcast.29, f32[16,64,512]{2,1,0:T(8,128)S(1)} %copy-done, f32[16,64,512]{2,1,0:T(8,128)S(1)} %copy-done.25), custom_call_target="tpu_custom_call" | custom-call | flops 10000000 | tf_op jit(solution)/shard_map/pair/pallas_call | solution.py:496
  35.6 4.3 %collective-permute-start.3 = (f32[4,64,512]{2,1,0:T(8,128)S(1)}, f32[4,64,512]{2,1,0:T(8,128)S(1)}, u32[]{:S(2)}, u32[]{:S(2)}) collective-permute-start(f32[4,64,512]{2,1,0:T(8,128)S(1)} %pair.4.other), channel_id=1, source_target_pairs={{0,1},{1,0},{2,3},{3,2},{4,5},{5,4},{6,7},{7,6},{8,9},{9,8},{10,11... | collective-permute-start | bytes 1572872 | tf_op jit(solution)/shard_map/ppermute | solution.py:414
  40.0 1.8 %cross.4 = (f32[16,64,512]{2,1,0:T(8,128)S(1)}, f32[4,64,512]{2,1,0:T(8,128)S(1)}) custom-call(s32[1]{0:T(128)} %bitcast.7.place, f32[16,64,512]{2,1,0:T(8,128)S(1)} %bitcast.22, f32[4,64,512]{2,1,0:T(8,128)S(1)} %collective-permute-done.halo, f32[16,64,512]{2,1,0:T(8,128)S(1)} %bitcast.30, f32[16,64,512]{2,1,0:T(8,128)S(1)} %copy-done, ...), custom_call_target="tpu_custom_call" | custom-call | flops 10000000 | tf_op jit(solution)/shard_map/cross/pallas_call | solution.py:499
  42.5 3.0 %inner.5.middle = f32[8,64,512]{2,1,0:T(8,128)S(1)} custom-call(f32[16,64,512]{2,1,0:T(8,128)S(1)} %get-tuple-element.24.now.w1.later, f32[16,64,512]{2,1,0:T(8,128)S(1)} %bitcast.23, f32[16,64,512]{2,1,0:T(8,128)S(1)} %copy-done, f32[16,64,512]{2,1,0:T(8,128)S(1)} %copy-done.23), custom_call_target="tpu_custom_call" | custom-call | flops 15000000 | tf_op jit(solution)/shard_map/inner/pallas_call | solution.py:495
  45.4 16.7 %collective-permute-done.3.halo = f32[4,64,512]{2,1,0:T(8,128)S(1)} collective-permute-done((f32[4,64,512]{2,1,0:T(8,128)S(1)}, f32[4,64,512]{2,1,0:T(8,128)S(1)}, u32[]{:S(2)}, u32[]{:S(2)}) %collective-permute-start.3) | collective-permute-done | bytes 524320 | tf_op jit(solution)/shard_map/ppermute | solution.py:414
  63.7 2.5 %collective-permute-start.5 = (f32[4,64,512]{2,1,0:T(8,128)S(1)}, f32[4,64,512]{2,1,0:T(8,128)S(1)}, u32[]{:S(2)}, u32[]{:S(2)}) collective-permute-start(f32[4,64,512]{2,1,0:T(8,128)S(1)} %pair.5.other), channel_id=1, source_target_pairs={{0,1},{1,0},{2,3},{3,2},{4,5},{5,4},{6,7},{7,6},{8,9},{9,8},{10,11... | collective-permute-start | bytes 1572872 | tf_op jit(solution)/shard_map/ppermute | solution.py:414
  66.2 2.6 %cross.5 = (f32[16,64,512]{2,1,0:T(8,128)S(1)}, f32[4,64,512]{2,1,0:T(8,128)}) custom-call(s32[1]{0:T(128)} %bitcast.7.place, f32[16,64,512]{2,1,0:T(8,128)S(1)} %get-tuple-element.24.now.w1.later, f32[4,64,512]{2,1,0:T(8,128)S(1)} %collective-permute-done.2.halo, f32[16,64,512]{2,1,0:T(8,128)S(1)} %bitcast.25, f32[16,64,512]{2,1,0:T(8,128)S(1)} %copy-done, ...), custom_call_target="tpu_custom_call" | custom-call | flops 10000000 | tf_op jit(solution)/shard_map/cross/pallas_call | solution.py:499
  71.6 1.6 %copy-done.6 = f32[16,64,512]{2,1,0:T(8,128)S(1)} copy-done((f32[16,64,512]{2,1,0:T(8,128)S(1)}, f32[16,64,512]{2,1,0:T(8,128)}, u32[]{:S(2)}) %copy-start.6) | copy-done | bytes 2097176
  73.2 1.6 %copy-done.10 = f32[16,64,512]{2,1,0:T(8,128)S(1)} copy-done((f32[16,64,512]{2,1,0:T(8,128)S(1)}, f32[16,64,512]{2,1,0:T(8,128)}, u32[]{:S(2)}) %copy-start.10) | copy-done | bytes 2097176
  74.8 1.6 %copy-done.20 = f32[16,64,512]{2,1,0:T(8,128)S(1)} copy-done((f32[16,64,512]{2,1,0:T(8,128)S(1)}, f32[16,64,512]{2,1,0:T(8,128)}, u32[]{:S(2)}) %copy-start.20) | copy-done | bytes 2097176
  76.4 3.0 %inner.6.middle = f32[8,64,512]{2,1,0:T(8,128)S(1)} custom-call(f32[16,64,512]{2,1,0:T(8,128)S(1)} %copy-done.6, f32[16,64,512]{2,1,0:T(8,128)S(1)} %copy-done.10, f32[16,64,512]{2,1,0:T(8,128)S(1)} %copy-done, f32[16,64,512]{2,1,0:T(8,128)S(1)} %copy-done.20), custom_call_target="tpu_custom_call" | custom-call | flops 15000000 | tf_op jit(solution)/shard_map/inner/pallas_call | solution.py:495
  80.2 7.5 %image.1 = (f32[16,64,512]{2,1,0:T(8,128)S(1)}, f32[16,64,512]{2,1,0:T(8,128)S(1)}) custom-call(s32[1]{0:T(128)} %bitcast.2.first, s32[1,3]{1,0:T(1,128)S(1)} %copy-done.36, s32[6,16,64,128]{3,2,1,0:T(8,128)S(1)} %bitcast.32, s32[6,16,256]{2,1,0:T(8,128)S(1)} %bitcast.36, f32[1,64]{1,0:T(1,128)S(1)} %bitcast.39, f32[16,64,512]{2,1,0:T(8,128)S(1)} %bitcast.26, ...), custom_call_target="tpu_custom_call" | custom-call | flops 25000000 | tf_op jit(solution)/shard_map/image/pallas_call | solution.py:530
  87.7 1.6 %pair.6.other = f32[4,64,512]{2,1,0:T(8,128)S(1)} custom-call(s32[1]{0:T(128)} %bitcast.11.place, f32[16,64,512]{2,1,0:T(8,128)S(1)} %copy-done.7, f32[4,64,512]{2,1,0:T(8,128)S(1)} %collective-permute-done.5.halo, f32[16,64,512]{2,1,0:T(8,128)S(1)} %copy-done.11, f32[16,64,512]{2,1,0:T(8,128)S(1)} %copy-done, f32[16,64,512]{2,1,0:T(8,128)S(1)} %copy-done.21), custom_call_target="tpu_custom_call" | custom-call | flops 10000000 | tf_op jit(solution)/shard_map/pair/pallas_call | solution.py:496
  89.3 4.1 %cross.6 = (f32[16,64,512]{2,1,0:T(8,128)}, f32[4,64,512]{2,1,0:T(8,128)S(1)}) custom-call(s32[1]{0:T(128)} %bitcast.7.place, f32[16,64,512]{2,1,0:T(8,128)S(1)} %copy-done.7, f32[4,64,512]{2,1,0:T(8,128)} %collective-permute-done.4.halo, f32[16,64,512]{2,1,0:T(8,128)S(1)} %copy-done.11, f32[16,64,512]{2,1,0:T(8,128)S(1)} %copy-done, ...), custom_call_target="tpu_custom_call" | custom-call | flops 10000000 | tf_op jit(solution)/shard_map/cross/pallas_call | solution.py:499
  94.2 1.6 %copy-done.12 = f32[16,64,512]{2,1,0:T(8,128)S(1)} copy-done((f32[16,64,512]{2,1,0:T(8,128)S(1)}, f32[16,64,512]{2,1,0:T(8,128)}, u32[]{:S(2)}) %copy-start.12) | copy-done | bytes 2097176
  98.2 3.6 %collective-permute-start.9 = (f32[4,64,512]{2,1,0:T(8,128)S(1)}, f32[4,64,512]{2,1,0:T(8,128)S(1)}, u32[]{:S(2)}, u32[]{:S(2)}) collective-permute-start(f32[4,64,512]{2,1,0:T(8,128)S(1)} %pair.6.other), channel_id=1, source_target_pairs={{0,1},{1,0},{2,3},{3,2},{4,5},{5,4},{6,7},{7,6},{8,9},{9,8},{10,11... | collective-permute-start | bytes 1572872 | tf_op jit(solution)/shard_map/ppermute | solution.py:414
  107.6 3.5 %collective-permute-start.10 = (f32[8,128]{1,0:T(8,128)S(1)}, f32[8,128]{1,0:T(8,128)S(1)}, u32[]{:S(2)}, u32[]{:S(2)}) collective-permute-start(f32[8,128]{1,0:T(8,128)S(1)} %get-tuple-element.22.after.one), channel_id=1, source_target_pairs={{0,1},{1,0},{2,3},{3,2},{4,5},{5,4},{6,7},{7,6},{8,9},{9,8},{10,11... | collective-permute-start | bytes 12296 | tf_op jit(solution)/shard_map/ppermute | solution.py:366
  111.1 13.8 %collective-permute-done.10.other = f32[8,128]{1,0:T(8,128)S(1)} collective-permute-done((f32[8,128]{1,0:T(8,128)S(1)}, f32[8,128]{1,0:T(8,128)S(1)}, u32[]{:S(2)}, u32[]{:S(2)}) %collective-permute-start.10) | collective-permute-done | bytes 4128 | tf_op jit(solution)/shard_map/ppermute | solution.py:366
  125.0 3.7 %collective-permute-start.11 = (f32[8,128]{1,0:T(8,128)S(1)}, f32[8,128]{1,0:T(8,128)S(1)}, u32[]{:S(2)}, u32[]{:S(2)}) collective-permute-start(f32[8,128]{1,0:T(8,128)S(1)} %tally.5.one), channel_id=1, source_target_pairs={{0,2},{1,3},{2,0},{3,1},{4,6},{5,7},{6,4},{7,5},{8,10},{9,11},{10,... | collective-permute-start | bytes 12296 | tf_op jit(solution)/shard_map/ppermute | solution.py:366
  130.2 3.0 %collective-permute-start.12 = (f32[8,128]{1,0:T(8,128)S(1)}, f32[8,128]{1,0:T(8,128)S(1)}, u32[]{:S(2)}, u32[]{:S(2)}) collective-permute-start(f32[8,128]{1,0:T(8,128)S(1)} %tally.6.one), channel_id=1, source_target_pairs={{0,4},{1,5},{2,6},{3,7},{4,0},{5,1},{6,2},{7,3},{8,12},{9,13},{10,... | collective-permute-start | bytes 12296 | tf_op jit(solution)/shard_map/ppermute | solution.py:366
  137.5 2.1 %collective-permute-done.14.other = f32[8,128]{1,0:T(8,128)S(1)} collective-permute-done((f32[8,128]{1,0:T(8,128)S(1)}, f32[8,128]{1,0:T(8,128)S(1)}, u32[]{:S(2)}, u32[]{:S(2)}) %collective-permute-start.14) | collective-permute-done | bytes 4128 | tf_op jit(solution)/shard_map/ppermute | solution.py:366
  141.8 1.6 %copy-done.18 = f32[16,64,512]{2,1,0:T(8,128)S(1)} copy-done((f32[16,64,512]{2,1,0:T(8,128)S(1)}, f32[16,64,512]{2,1,0:T(8,128)}, u32[]{:S(2)}) %copy-start.18) | copy-done | bytes 2097176
  143.4 3.0 %inner.7.middle = f32[8,64,512]{2,1,0:T(8,128)S(1)} custom-call(f32[16,64,512]{2,1,0:T(8,128)S(1)} %copy-done.13, f32[16,64,512]{2,1,0:T(8,128)S(1)} %copy-done.8, f32[16,64,512]{2,1,0:T(8,128)S(1)} %copy-done, f32[16,64,512]{2,1,0:T(8,128)S(1)} %copy-done.18), custom_call_target="tpu_custom_call" | custom-call | flops 15000000 | tf_op jit(solution)/shard_map/inner/pallas_call | solution.py:495
  146.4 1.6 %pair.7.other = f32[4,64,512]{2,1,0:T(8,128)S(1)} custom-call(s32[1]{0:T(128)} %bitcast.11.place, f32[16,64,512]{2,1,0:T(8,128)S(1)} %copy-done.13, f32[4,64,512]{2,1,0:T(8,128)S(1)} %collective-permute-done.9.halo, f32[16,64,512]{2,1,0:T(8,128)S(1)} %copy-done.8, f32[16,64,512]{2,1,0:T(8,128)S(1)} %copy-done, f32[16,64,512]{2,1,0:T(8,128)S(1)} %copy-done.18), custom_call_target="tpu_custom_call" | custom-call | flops 10000000 | tf_op jit(solution)/shard_map/pair/pallas_call | solution.py:496
  148.0 4.3 %cross.7 = (f32[16,64,512]{2,1,0:T(8,128)}, f32[4,64,512]{2,1,0:T(8,128)}) custom-call(s32[1]{0:T(128)} %bitcast.7.place, f32[16,64,512]{2,1,0:T(8,128)S(1)} %copy-done.14, f32[4,64,512]{2,1,0:T(8,128)} %collective-permute-done.8.halo, f32[16,64,512]{2,1,0:T(8,128)S(1)} %copy-done.8, f32[16,64,512]{2,1,0:T(8,128)S(1)} %copy-done, ...), custom_call_target="tpu_custom_call" | custom-call | flops 10000000 | tf_op jit(solution)/shard_map/cross/pallas_call | solution.py:499
  (98 shorter events, 35.5 us)
Async XLA Ops:
  1.7 32.3 %collective-permute-start.1 = (f32[4,64,512]{2,1,0:T(8,128)S(1)}, f32[4,64,512]{2,1,0:T(8,128)S(1)}, u32[]{:S(2)}, u32[]{:S(2)}) collective-permute-start(f32[4,64,512]{2,1,0:T(8,128)S(1)} %dynamic-slice_bitcast_fusion), channel_id=1, source_target_pairs={{0,1},{1,0},{2,3},{3,2},{4,5},{5,4},{6,7},{7,6},{8,9},{9,8},{10,11... | collective-permute-start | bytes 1572872 | tf_op jit(solution)/shard_map/ppermute | solution.py:414
  4.8 1.9 %copy-start.26 = (s32[1,6,16,64,128]{4,3,2,1,0:T(8,128)S(1)}, s32[1,6,16,64,128]{4,3,2,1,0:T(8,128)}, u32[]{:S(2)}) copy-start(s32[1,6,16,64,128]{4,3,2,1,0:T(8,128)} %param.12) | copy-start | bytes 9437188
  23.7 2.5 %copy-start = (f32[16,64,512]{2,1,0:T(8,128)S(1)}, f32[16,64,512]{2,1,0:T(8,128)}, u32[]{:S(2)}) copy-start(f32[16,64,512]{2,1,0:T(8,128)} %courant.23) | copy-start | bytes 6291460
  23.7 1.7 %copy-start.1 = (f32[1,16,64,512]{3,2,1,0:T(8,128)S(1)}, f32[1,16,64,512]{3,2,1,0:T(8,128)}, u32[]{:S(2)}) copy-start(f32[1,16,64,512]{3,2,1,0:T(8,128)} %param.9) | copy-start | bytes 6291460
  25.5 14.4 %collective-permute-start = (f32[4,64,512]{2,1,0:T(8,128)S(1)}, f32[4,64,512]{2,1,0:T(8,128)S(1)}, u32[]{:S(2)}, u32[]{:S(2)}) collective-permute-start(f32[4,64,512]{2,1,0:T(8,128)S(1)} %cut.1), channel_id=1, source_target_pairs={{1,2},{3,4},{5,6},{2,1},{4,3},{6,5},{9,10},{11,12},{13,14},{10,9},... | collective-permute-start | bytes 1572872 | tf_op jit(solution)/shard_map/ppermute | solution.py:417
  34.0 6.0 %copy-start.3 = (f32[1,16,64,512]{3,2,1,0:T(8,128)S(1)}, f32[1,16,64,512]{3,2,1,0:T(8,128)}, u32[]{:S(2)}) copy-start(f32[1,16,64,512]{3,2,1,0:T(8,128)} %param.9) | copy-start | bytes 6291460
  34.0 6.0 %copy-start.16 = (f32[1,16,64,512]{3,2,1,0:T(8,128)S(1)}, f32[1,16,64,512]{3,2,1,0:T(8,128)}, u32[]{:S(2)}) copy-start(f32[1,16,64,512]{3,2,1,0:T(8,128)} %param.10) | copy-start | bytes 6291460
  35.6 6.8 %copy-start.23 = (f32[16,64,512]{2,1,0:T(8,128)S(1)}, f32[16,64,512]{2,1,0:T(8,128)}, u32[]{:S(2)}) copy-start(f32[16,64,512]{2,1,0:T(8,128)} %copy-done.22) | copy-start | bytes 6291460
  35.6 26.5 %collective-permute-start.3 = (f32[4,64,512]{2,1,0:T(8,128)S(1)}, f32[4,64,512]{2,1,0:T(8,128)S(1)}, u32[]{:S(2)}, u32[]{:S(2)}) collective-permute-start(f32[4,64,512]{2,1,0:T(8,128)S(1)} %pair.4.other), channel_id=1, source_target_pairs={{0,1},{1,0},{2,3},{3,2},{4,5},{5,4},{6,7},{7,6},{8,9},{9,8},{10,11... | collective-permute-start | bytes 1572872 | tf_op jit(solution)/shard_map/ppermute | solution.py:414
  41.7 24.5 %copy-start.9 = (f32[16,64,512]{2,1,0:T(8,128)}, f32[16,64,512]{2,1,0:T(8,128)S(1)}, u32[]{:S(2)}) copy-start(f32[16,64,512]{2,1,0:T(8,128)S(1)} %get-tuple-element.24.now.w1.later) | copy-start | bytes 6291460
  41.8 24.5 %collective-permute-start.2 = (f32[4,64,512]{2,1,0:T(8,128)S(1)}, f32[4,64,512]{2,1,0:T(8,128)S(1)}, u32[]{:S(2)}, u32[]{:S(2)}) collective-permute-start(f32[4,64,512]{2,1,0:T(8,128)S(1)} %get-tuple-element.25), channel_id=1, source_target_pairs={{1,2},{3,4},{5,6},{2,1},{4,3},{6,5},{9,10},{11,12},{13,14},{10,9},... | collective-permute-start | bytes 1572872 | tf_op jit(solution)/shard_map/ppermute | solution.py:417
  63.7 23.9 %collective-permute-start.5 = (f32[4,64,512]{2,1,0:T(8,128)S(1)}, f32[4,64,512]{2,1,0:T(8,128)S(1)}, u32[]{:S(2)}, u32[]{:S(2)}) collective-permute-start(f32[4,64,512]{2,1,0:T(8,128)S(1)} %pair.5.other), channel_id=1, source_target_pairs={{0,1},{1,0},{2,3},{3,2},{4,5},{5,4},{6,7},{7,6},{8,9},{9,8},{10,11... | collective-permute-start | bytes 1572872 | tf_op jit(solution)/shard_map/ppermute | solution.py:414
  66.2 13.2 %copy-start.31 = (s32[1,6,16,256]{3,2,1,0:T(8,128)S(1)}, s32[1,6,16,256]{3,2,1,0:T(8,128)}, u32[]{:S(2)}) copy-start(s32[1,6,16,256]{3,2,1,0:T(8,128)} %param.13) | copy-start | bytes 294916
  70.2 19.1 %collective-permute-start.4 = (f32[4,64,512]{2,1,0:T(8,128)}, f32[4,64,512]{2,1,0:T(8,128)}, u32[]{:S(2)}, u32[]{:S(2)}) collective-permute-start(f32[4,64,512]{2,1,0:T(8,128)} %get-tuple-element.30), channel_id=1, source_target_pairs={{1,2},{3,4},{5,6},{2,1},{4,3},{6,5},{9,10},{11,12},{13,14},{10,9},... | collective-permute-start | bytes 1572872 | tf_op jit(solution)/shard_map/ppermute | solution.py:417
  76.4 3.0 %copy-start.4 = (f32[1,16,64,512]{3,2,1,0:T(8,128)S(1)}, f32[1,16,64,512]{3,2,1,0:T(8,128)}, u32[]{:S(2)}) copy-start(f32[1,16,64,512]{3,2,1,0:T(8,128)} %param.9) | copy-start | bytes 6291460
  76.4 3.0 %copy-start.7 = (f32[16,64,512]{2,1,0:T(8,128)S(1)}, f32[16,64,512]{2,1,0:T(8,128)}, u32[]{:S(2)}) copy-start(f32[16,64,512]{2,1,0:T(8,128)} %copy-done.5) | copy-start | bytes 6291460
  76.4 3.0 %copy-start.11 = (f32[16,64,512]{2,1,0:T(8,128)S(1)}, f32[16,64,512]{2,1,0:T(8,128)}, u32[]{:S(2)}) copy-start(f32[16,64,512]{2,1,0:T(8,128)} %copy-done.9) | copy-start | bytes 6291460
  76.4 3.8 %copy-start.27 = (s32[1,6,16,64,128]{4,3,2,1,0:T(8,128)S(1)}, s32[1,6,16,64,128]{4,3,2,1,0:T(8,128)}, u32[]{:S(2)}) copy-start(s32[1,6,16,64,128]{4,3,2,1,0:T(8,128)} %param.12) | copy-start | bytes 9437188
  76.4 3.8 %copy-start.34 = (f32[64]{0:T(128)S(1)}, f32[64]{0:T(128)}, u32[]{:S(2)}) copy-start(f32[64]{0:T(128)} %param.14) | copy-start | bytes 772
  76.4 3.7 %copy-start.36 = (s32[1,3]{1,0:T(1,128)S(1)}, s32[1,3]{1,0:T(1,128)}, u32[]{:S(2)}) copy-start(s32[1,3]{1,0:T(1,128)} %source.1) | copy-start | bytes 40
  80.2 7.5 %copy-start.21 = (f32[16,64,512]{2,1,0:T(8,128)S(1)}, f32[16,64,512]{2,1,0:T(8,128)}, u32[]{:S(2)}) copy-start(f32[16,64,512]{2,1,0:T(8,128)} %copy-done.19) | copy-start | bytes 6291460
  98.2 5.1 %collective-permute-start.6 = (f32[2,16,16,512]{3,2,1,0:T(8,128)}, f32[2,16,16,512]{3,2,1,0:T(8,128)}, u32[]{:S(2)}, u32[]{:S(2)}) collective-permute-start(f32[2,16,16,512]{3,2,1,0:T(8,128)} %get-tuple-element.34), channel_id=1, source_target_pairs={{0,8},{8,0},{16,24},{24,16},{1,9},{9,1},{17,25},{25,17},{2,10},{10... | collective-permute-start | bytes 3145736 | tf_op jit(solution)/shard_map/ppermute | solution.py:555
  98.2 48.2 %collective-permute-start.9 = (f32[4,64,512]{2,1,0:T(8,128)S(1)}, f32[4,64,512]{2,1,0:T(8,128)S(1)}, u32[]{:S(2)}, u32[]{:S(2)}) collective-permute-start(f32[4,64,512]{2,1,0:T(8,128)S(1)} %pair.6.other), channel_id=1, source_target_pairs={{0,1},{1,0},{2,3},{3,2},{4,5},{5,4},{6,7},{7,6},{8,9},{9,8},{10,11... | collective-permute-start | bytes 1572872 | tf_op jit(solution)/shard_map/ppermute | solution.py:414
  101.8 46.2 %collective-permute-start.8 = (f32[4,64,512]{2,1,0:T(8,128)}, f32[4,64,512]{2,1,0:T(8,128)}, u32[]{:S(2)}, u32[]{:S(2)}) collective-permute-start(f32[4,64,512]{2,1,0:T(8,128)} %copy-done.37), channel_id=1, source_target_pairs={{1,2},{3,4},{5,6},{2,1},{4,3},{6,5},{9,10},{11,12},{13,14},{10,9},... | collective-permute-start | bytes 1572872 | tf_op jit(solution)/shard_map/ppermute | solution.py:417
  103.2 37.0 %copy-start.8 = (f32[16,64,512]{2,1,0:T(8,128)S(1)}, f32[16,64,512]{2,1,0:T(8,128)}, u32[]{:S(2)}) copy-start(f32[16,64,512]{2,1,0:T(8,128)} %copy-done.5) | copy-start | bytes 6291460
  106.0 46.3 %collective-permute-start.7 = (f32[1,16,16,512]{3,2,1,0:T(8,128)S(1)}, f32[1,16,16,512]{3,2,1,0:T(8,128)S(1)}, u32[]{:S(2)}, u32[]{:S(2)}) collective-permute-start(f32[1,16,16,512]{3,2,1,0:T(8,128)S(1)} %get-tuple-element.36), channel_id=1, source_target_pairs={{0,16},{8,24},{16,0},{24,8},{1,17},{9,25},{17,1},{25,9},{2,18},{10... | collective-permute-start | bytes 1572872 | tf_op jit(solution)/shard_map/ppermute | solution.py:555
  107.6 17.4 %collective-permute-start.10 = (f32[8,128]{1,0:T(8,128)S(1)}, f32[8,128]{1,0:T(8,128)S(1)}, u32[]{:S(2)}, u32[]{:S(2)}) collective-permute-start(f32[8,128]{1,0:T(8,128)S(1)} %get-tuple-element.22.after.one), channel_id=1, source_target_pairs={{0,1},{1,0},{2,3},{3,2},{4,5},{5,4},{6,7},{7,6},{8,9},{9,8},{10,11... | collective-permute-start | bytes 12296 | tf_op jit(solution)/shard_map/ppermute | solution.py:366
  125.0 5.3 %collective-permute-start.11 = (f32[8,128]{1,0:T(8,128)S(1)}, f32[8,128]{1,0:T(8,128)S(1)}, u32[]{:S(2)}, u32[]{:S(2)}) collective-permute-start(f32[8,128]{1,0:T(8,128)S(1)} %tally.5.one), channel_id=1, source_target_pairs={{0,2},{1,3},{2,0},{3,1},{4,6},{5,7},{6,4},{7,5},{8,10},{9,11},{10,... | collective-permute-start | bytes 12296 | tf_op jit(solution)/shard_map/ppermute | solution.py:366
  130.2 4.6 %collective-permute-start.12 = (f32[8,128]{1,0:T(8,128)S(1)}, f32[8,128]{1,0:T(8,128)S(1)}, u32[]{:S(2)}, u32[]{:S(2)}) collective-permute-start(f32[8,128]{1,0:T(8,128)S(1)} %tally.6.one), channel_id=1, source_target_pairs={{0,4},{1,5},{2,6},{3,7},{4,0},{5,1},{6,2},{7,3},{8,12},{9,13},{10,... | collective-permute-start | bytes 12296 | tf_op jit(solution)/shard_map/ppermute | solution.py:366
  134.9 1.2 collective-permute-start.13
  136.0 3.6 %collective-permute-start.14 = (f32[8,128]{1,0:T(8,128)S(1)}, f32[8,128]{1,0:T(8,128)S(1)}, u32[]{:S(2)}, u32[]{:S(2)}) collective-permute-start(f32[8,128]{1,0:T(8,128)S(1)} %tally.8.one), channel_id=1, source_target_pairs={{0,16},{8,24},{16,0},{24,8},{1,17},{9,25},{17,1},{25,9},{2,18},{10... | collective-permute-start | bytes 12296 | tf_op jit(solution)/shard_map/ppermute | solution.py:366
  146.4 1.6 %copy-start.14 = (f32[16,64,512]{2,1,0:T(8,128)S(1)}, f32[16,64,512]{2,1,0:T(8,128)}, u32[]{:S(2)}) copy-start(f32[16,64,512]{2,1,0:T(8,128)} %get-tuple-element.32.w3.now) | copy-start | bytes 6291460
  (21 other events, 27.1 us)
